TPU v7x, 32 devices: a whole 2x2x4 slice. The times are simulated.
32 devices in a mesh: tm: 4 (over y, core), space: 8 (over z, x).
Axes of the slice: x: 2, y: 2, z: 4, core: 2. Of those that a mesh axis runs over, the one named last changes fastest.
Arguments:
- perm_field: float32 [4, 32, 32, 256], P(None, 'space'), may hold values from 0.5 to 2
- step_multiplier: float32 [4, 32, 32, 256], P('tm', 'space'), may hold values from 0.5 to 2
- inflow: float32 [4, 32, 32, 256], P('tm', 'space'), may hold values from -3 to 3
- start_pressure: float32 [32, 32, 256], P('space'), may hold values from -6 to 6
- start_saturation: float32 [32, 32, 256], P('space'), may hold values from 0.1 to 0.9
- region_ids: int32 [32, 32, 256], P('space'), may hold values from 0 to 7
- region_table: float32 [3, 8], replicated, may hold values from 0.25 to 2
- well_cells: int32 [32], replicated, may hold values from 0 to 262143
- well_rates: float32 [4, 32], P('tm'), may hold values from -8 to 8
- observed: float32 [4, 4, 32], P(None, 'tm'), may hold values from -6 to 6
Outputs:
- misfit: float32 [4], replicated
- slab_pressure: float32 [4, 4, 32, 32, 256], P('tm', None, 'space')
- slab_saturation: float32 [4, 4, 32, 32, 256], P('tm', None, 'space')
All inputs are finite; a program needn't handle non-finite values.
Results may differ from a plain program's by a relative error of at most 0.0003.
Values sent between devices are 32-bit elements; how exact they have to be, the bound alone decides.
A program may use at most 64 MiB of HBM per device.

v0:
```python
import jax
import jax.numpy as jnp
from jax import lax
from jax.sharding import PartitionSpec as P

MB = 1
REP_DEV = 1
ITERS = 3


def padded(cells, sides, width):
    for axis, dim in sides:
        count = lax.axis_size(axis)
        ends = count - 1
        head = lax.slice_in_dim(cells, 0, width, axis=dim)
        tail = lax.slice_in_dim(cells, cells.shape[dim] - width, cells.shape[dim], axis=dim)
        cells = jnp.concatenate(
            [
                lax.ppermute(tail, axis, [(i, (i + 1) % count) for i in range(ends)]),
                cells,
                lax.ppermute(head, axis, [((i + 1) % count, i) for i in range(ends)]),
            ],
            axis=dim,
        )
    return cells


def shifted(values, dimension, offset):
    margins = [(0, 0)] * values.ndim
    length = values.shape[dimension]
    if offset > 0:
        margins[dimension] = (1, 0)
        return lax.slice_in_dim(jnp.pad(values, margins), 0, length, axis=dimension)
    margins[dimension] = (0, 1)
    return lax.slice_in_dim(jnp.pad(values, margins), 1, length + 1, axis=dimension)


def neighbour_values(values_ext):
    middle = values_ext[:, 1:-1]
    return (
        values_ext[:, :-2],
        values_ext[:, 2:],
        shifted(middle, 2, 1),
        shifted(middle, 2, -1),
        shifted(middle, 3, 1),
        shifted(middle, 3, -1),
    )


def coefficients(conduct_ext):
    middle = conduct_ext[:, 1:-1]
    others = neighbour_values(conduct_ext)
    links = [jnp.sqrt(middle * other_side) for other_side in others]
    link_total = links[0] + links[1] + links[2] + links[3] + links[4] + links[5]
    return tuple(links) + (link_total,)


def jacobi_sweep(pressure_ext, couplings, storage, right_side):
    beside = neighbour_values(pressure_ext)
    inflowing = couplings[0] * beside[0]
    for link_index in range(1, 6):
        inflowing = inflowing + couplings[link_index] * beside[link_index]
    divisor = jnp.where(storage > 0, storage + couplings[6], 1.0)
    return (right_side + inflowing) / divisor


def fraction(saturation, ratio):
    squared = saturation * saturation
    remain = (1.0 - saturation) * (1.0 - saturation)
    return squared / (squared + ratio * remain)


def transport(pressure_ext, flow_ext, couplings, saturation, gain, source):
    centre_p = pressure_ext[:, 1:-1]
    centre_f = flow_ext[:, 1:-1]
    other_p = neighbour_values(pressure_ext)
    other_f = neighbour_values(flow_ext)
    outflow = None
    for link_index in range(6):
        face_flux = couplings[link_index] * (centre_p - other_p[link_index])
        carried = face_flux * jnp.where(face_flux > 0, centre_f, other_f[link_index])
        outflow = carried if outflow is None else outflow + carried
    gained = (
        jnp.maximum(source, 0.0) * (1.0 - saturation)
        - jnp.maximum(-source, 0.0) * centre_f
        - outflow
    )
    return saturation + gain * gained


def region_fields(region_ids, region_table):
    fields = []
    for table_row in range(3):
        summed = jnp.zeros(region_ids.shape, jnp.float32)
        for region_index in range(region_table.shape[1]):
            summed = summed + jnp.where(
                region_ids == region_index, region_table[table_row, region_index], 0.0
            )
        fields.append(summed)
    return (fields[0], fields[1], 0.1 * fields[2])


def advance(pressure, saturation, conduct, source, inflow_now, storage, ratio, gain):
    right_side = storage * pressure + source + inflow_now
    flow_frac = fraction(saturation, ratio)
    edges = padded(jnp.stack([conduct, pressure]), (("space", 2),), 1)
    couplings = coefficients(edges[0])
    iterate_ext = edges[1]
    iterate = pressure
    for sweep_index in range(ITERS):
        if sweep_index > 0:
            iterate_ext = padded(iterate, (("space", 1),), 1)
        iterate = jacobi_sweep(iterate_ext, couplings, storage, right_side)
    both = padded(jnp.stack([iterate, flow_frac]), (("space", 2),), 1)
    saturation = transport(both[0], both[1], couplings, saturation, gain, source)
    return (iterate, saturation)


def body(
    perm_field,
    step_multiplier,
    inflow,
    start_pressure,
    start_saturation,
    region_ids,
    region_table,
    well_cells,
    well_rates,
    observed,
):
    sections = lax.axis_size("tm")
    section_index = lax.axis_index("tm")
    space_index = lax.axis_index("space")
    grid_shape = start_pressure.shape
    width_x, depth, across = grid_shape
    batch_size = MB
    storage, ratio, gain = region_fields(region_ids, region_table)
    layer_ids = lax.broadcasted_iota(jnp.int32, grid_shape, 0) + space_index * width_x
    cell_ids = (
        layer_ids * depth + lax.broadcasted_iota(jnp.int32, grid_shape, 1)
    ) * across + lax.broadcasted_iota(jnp.int32, grid_shape, 2)
    well_picks = (well_cells[:, None] == cell_ids.reshape(1, -1)).astype(jnp.float32)
    well_owned = jnp.sum(well_picks, axis=1)
    start_p = jnp.broadcast_to(start_pressure, (batch_size,) + grid_shape)
    start_s = jnp.broadcast_to(start_saturation, (batch_size,) + grid_shape)

    def mismatch(pressure, measured):
        predicted = jnp.dot(
            pressure.reshape(batch_size, -1), well_picks.T, precision=lax.Precision.HIGHEST
        )
        return jnp.sum(well_owned * (predicted - measured) ** 2, axis=1)

    misfit = jnp.zeros((perm_field.shape[0],), jnp.float32)
    fields = (
        lax.all_gather(step_multiplier, "tm", axis=0, tiled=True),
        lax.all_gather(inflow, "tm", axis=0, tiled=True),
        lax.all_gather(well_rates, "tm", axis=0, tiled=True),
    )
    measured_all = lax.all_to_all(observed, "tm", split_axis=0, concat_axis=1, tiled=True)
    perm_rows = lax.dynamic_slice_in_dim(perm_field, section_index * batch_size, batch_size, 0)
    rate_rows = fields[2]
    placed = jnp.dot(rate_rows, well_picks, precision=lax.Precision.HIGHEST)
    all_sources = placed.reshape((rate_rows.shape[0],) + grid_shape)
    zero_ends = jnp.zeros((sections, batch_size) + grid_shape, jnp.float32)

    def one_section(slab_index, state_tuple):
        pressure, saturation, ends_p, ends_s, errors = state_tuple
        position = slab_index * REP_DEV + 0
        multiplier = lax.dynamic_index_in_dim(fields[0], position, 0, keepdims=False)
        inflow_now = lax.dynamic_index_in_dim(fields[1], position, 0, keepdims=False)
        source = lax.dynamic_index_in_dim(all_sources, position, 0, keepdims=False)
        pressure, saturation = advance(
            pressure, saturation, perm_rows * multiplier, source, inflow_now, storage, ratio, gain
        )
        errors = errors + mismatch(
            pressure, lax.dynamic_index_in_dim(measured_all, position, 1, keepdims=False)
        )
        ends_p = lax.dynamic_update_index_in_dim(ends_p, pressure, slab_index, 0)
        ends_s = lax.dynamic_update_index_in_dim(ends_s, saturation, slab_index, 0)
        return (pressure, saturation, ends_p, ends_s, errors)

    result = lax.fori_loop(
        0,
        sections,
        one_section,
        (start_p, start_s, zero_ends, zero_ends, jnp.zeros((batch_size,), jnp.float32)),
    )
    slab_pressure, slab_saturation = (
        lax.all_to_all(result[2], "tm", split_axis=0, concat_axis=1, tiled=True),
        lax.all_to_all(result[3], "tm", split_axis=0, concat_axis=1, tiled=True),
    )
    misfit = lax.dynamic_update_slice_in_dim(misfit, result[4], section_index * batch_size, 0)
    totals = lax.psum(misfit, ("tm", "space"))
    return (totals / (sections * REP_DEV * well_cells.shape[0]), slab_pressure, slab_saturation)


def solution(mesh):
    return jax.shard_map(
        body,
        mesh=mesh,
        in_specs=(
            P(None, "space", None, None),
            P("tm", "space", None, None),
            P("tm", "space", None, None),
            P("space", None, None),
            P("space", None, None),
            P("space", None, None),
            P(),
            P(),
            P("tm", None),
            P(None, "tm", None),
        ),
        out_specs=(P(), P("tm", None, "space", None, None), P("tm", None, "space", None, None)),
        check_vma=False,
    )
```

profile of v0, /device:TPU:0, one launch (start us, length us, event | category | flops | bytes accessed | tf_op | source)
XLA Modules:
  0.0 281.1 jit_solution(10147886916045654952)
XLA Ops:
  0.7 4.4 %all-to-all-start = ((f32[4,1,32]{2,1,0:T(1,128)}), f32[4,1,32]{2,1,0:T(1,128)S(1)}, u32[]{:S(2)}, u32[]{:S(2)}) async-start(f32[4,1,32]{2,1,0:T(1,128)} %param.21), calls=%async_computation | async-start | bytes 4096 | tf_op jit(solution)/shard_map/all_to_all | solution.py:159
  6.7 5.2 %all-gather = f32[4,1,32]{2,1,0:T(1,128)S(1)} all-gather(f32[1,1,32]{2,1,0:T(1,128)S(1)} %bitcast.154), channel_id=1, replica_groups=mesh['tm'=4,'space'=8] {'tm'}, dimensions={0}, use_global_device_ids=true | all-gather | bytes 640 | tf_op jit(solution)/shard_map/all_gather | solution.py:157
  12.6 1.3 fusion.102
  13.9 8.2 %all_gather.10 = f32[4,4,32,256]{3,2,1,0:T(8,128)} all-gather(f32[1,4,32,256]{3,2,1,0:T(8,128)S(1)} %copy-done.7), channel_id=1, replica_groups=mesh['tm'=4,'space'=8] {'tm'}, dimensions={0}, use_global_device_ids=true | all-gather | bytes 655360 | tf_op jit(solution)/shard_map/all_gather | solution.py:156
  22.1 7.4 %all_gather.11 = f32[4,4,32,256]{3,2,1,0:T(8,128)S(1)} all-gather(f32[1,4,32,256]{3,2,1,0:T(8,128)S(1)} %copy-done.8), channel_id=1, replica_groups=mesh['tm'=4,'space'=8] {'tm'}, dimensions={0}, use_global_device_ids=true | all-gather | bytes 655360 | tf_op jit(solution)/shard_map/all_gather | solution.py:155
  29.6 5.2 %select_add_fusion = (f32[4,32,256]{2,1,0:T(8,128)S(1)}, pred[4,32,256]{2,1,0:T(8,128)(4,1)S(1)}, pred[4,32,256]{2,1,0:T(8,128)(4,1)S(1)}, pred[4,32,256]{2,1,0:...) fusion(f32[]{:T(128)} %bitcast.28, f32[]{:T(128)} %bitcast.27, ...), kind=kLoop, calls=%fused_computation.152 | loop fusion | flops 753664 | bytes 524320 | tf_op jit(solution)/shard_map/add | solution.py:96
  34.8 5.1 %add_multiply_fusion = f32[4,32,256]{2,1,0:T(8,128)S(1)} fusion(pred[4,32,256]{2,1,0:T(8,128)(4,1)S(1)} %get-tuple-element.474, pred[4,32,256]{2,1,0:T(8,128)(4,1)S(1)} %get-tuple-element.473, pred[4,32,256]{2,1,0:T(8,128)(4,1)S(1)} %get-tuple-element.472, pred[4,32,256]{2,1,0:T(8,128)(4,1)S(1)} %get-tuple-element.471, ...), kind=kLoop, calls=%fused_computation.153 | loop fusion | flops 524288 | bytes 393248 | tf_op jit(solution)/shard_map/mul | solution.py:100
  39.8 5.1 %select_add_fusion.1 = f32[4,32,256]{2,1,0:T(8,128)S(1)} fusion(pred[4,32,256]{2,1,0:T(8,128)(4,1)S(1)} %get-tuple-element.474, pred[4,32,256]{2,1,0:T(8,128)(4,1)S(1)} %get-tuple-element.473, pred[4,32,256]{2,1,0:T(8,128)(4,1)S(1)} %get-tuple-element.472, pred[4,32,256]{2,1,0:T(8,128)(4,1)S(1)} %get-tuple-element.471, ...), kind=kLoop, calls=%fused_computation.155 | loop fusion | flops 491520 | bytes 393248 | tf_op jit(solution)/shard_map/add | solution.py:96
  46.0 170.8 %while.24 = (s32[]{:T(128)}, f32[1,4,32,256]{3,2,1,0:T(8,128)S(1)}, f32[1,4,32,256]{3,2,1,0:T(8,128)S(1)}, f32[4,1,4,32,256]{4,3,2,1,0:T(8,128)}, f32[4,1,4,32,2...) while((s32[]{:T(128)}, f32[1,4,32,256]{3,2,1,0:T(8,128)S(1)}, ...), condition=%wide.region_3.4_spmd.clone, body=%wide.region_1.3_spmd.clone.sunk | while | flops 19529856 | bytes 16516069 | solution.py:182
  46.0 1.3 collective-permute-start
  47.3 4.5 %collective-permute-start.1 = (f32[2,1,1,32,256]{4,3,2,1,0:T(8,128)S(1)}, f32[2,1,1,32,256]{4,3,2,1,0:T(8,128)S(1)}, u32[]{:S(2)}, u32[]{:S(2)}) collective-permute-start(f32[2,1,1,32,256]{4,3,2,1,0:T(8,128)S(1)} %get-tuple-element.644), channel_id=1, source_target_pairs={{0,1},{1,2},{2,3},{3,4},{4,5},{5,6},{6,7},{8,9},{9,10},{10,11},{11... | collective-permute-start | bytes 196616 | tf_op jit(solution)/shard_map/while/body/eval_jaxpr/ppermute | solution.py:19
  52.4 1.6 collective-permute-done.1
  54.1 1.3 fusion.133
  55.4 1.3 collective-permute-start.2
  56.7 5.1 %collective-permute-start.3 = (f32[1,1,32,256]{3,2,1,0:T(8,128)S(1)}, f32[1,1,32,256]{3,2,1,0:T(8,128)S(1)}, u32[]{:S(2)}, u32[]{:S(2)}) collective-permute-start(f32[1,1,32,256]{3,2,1,0:T(8,128)S(1)} %get-tuple-element.656), channel_id=1, source_target_pairs={{0,1},{1,2},{2,3},{3,4},{4,5},{5,6},{6,7},{8,9},{9,10},{10,11},{11... | collective-permute-start | bytes 98312 | tf_op jit(solution)/shard_map/while/body/eval_jaxpr/ppermute | solution.py:19
  61.8 1.6 collective-permute-done.3
  63.6 1.3 collective-permute-start.4
  64.9 5.8 %collective-permute-start.5 = (f32[1,1,32,256]{3,2,1,0:T(8,128)S(1)}, f32[1,1,32,256]{3,2,1,0:T(8,128)S(1)}, u32[]{:S(2)}, u32[]{:S(2)}) collective-permute-start(f32[1,1,32,256]{3,2,1,0:T(8,128)S(1)} %get-tuple-element.658), channel_id=1, source_target_pairs={{0,1},{1,2},{2,3},{3,4},{4,5},{5,6},{6,7},{8,9},{9,10},{10,11},{11... | collective-permute-start | bytes 98312 | tf_op jit(solution)/shard_map/while/body/eval_jaxpr/ppermute | solution.py:19
  70.7 1.6 collective-permute-done.5
  72.9 1.6 constant_dynamic-update-slice_fusion.2
  74.4 1.4 collective-permute-start.6
  75.9 5.8 %collective-permute-start.7 = (f32[2,1,1,32,256]{4,3,2,1,0:T(8,128)S(1)}, f32[2,1,1,32,256]{4,3,2,1,0:T(8,128)S(1)}, u32[]{:S(2)}, u32[]{:S(2)}) collective-permute-start(f32[2,1,1,32,256]{4,3,2,1,0:T(8,128)S(1)} %get-tuple-element.662), channel_id=1, source_target_pairs={{0,1},{1,2},{2,3},{3,4},{4,5},{5,6},{6,7},{8,9},{9,10},{10,11},{11... | collective-permute-start | bytes 196616 | tf_op jit(solution)/shard_map/while/body/eval_jaxpr/ppermute | solution.py:19
  81.8 4.0 %fusion.137 = f32[]{:T(128)} fusion(f32[32]{0:T(128)S(1)} %get-tuple-element.718, f32[32768,1]{0,1:T(1,128)S(1)} %bitcast.144, s32[32768]{0:T(1024)S(1)} %copy-done.6, s32[32]{0:T(128)S(1)} %get-tuple-element.720, f32[1,4,32]{2,1,0:T(4,128)S(1)} %get-tuple-element.717, s32[]{:T(128)S(6)} %copy.28), kind=kOutput, calls=%fused_computation.10.clone.1 | convolution fusion | flops 14680191 | bytes 262536 | tf_op jit(solution)/shard_map/while/body/eval_jaxpr/dot_general | solution.py:148
  87.6 1.3 collective-permute-start
  88.9 5.8 %collective-permute-start.1 = (f32[2,1,1,32,256]{4,3,2,1,0:T(8,128)S(1)}, f32[2,1,1,32,256]{4,3,2,1,0:T(8,128)S(1)}, u32[]{:S(2)}, u32[]{:S(2)}) collective-permute-start(f32[2,1,1,32,256]{4,3,2,1,0:T(8,128)S(1)} %get-tuple-element.644), channel_id=1, source_target_pairs={{0,1},{1,2},{2,3},{3,4},{4,5},{5,6},{6,7},{8,9},{9,10},{10,11},{11... | collective-permute-start | bytes 196616 | tf_op jit(solution)/shard_map/while/body/eval_jaxpr/ppermute | solution.py:19
  95.0 1.6 collective-permute-done.1
  96.7 1.3 fusion.133
  98.0 1.3 collective-permute-start.2
  99.3 5.4 %collective-permute-start.3 = (f32[1,1,32,256]{3,2,1,0:T(8,128)S(1)}, f32[1,1,32,256]{3,2,1,0:T(8,128)S(1)}, u32[]{:S(2)}, u32[]{:S(2)}) collective-permute-start(f32[1,1,32,256]{3,2,1,0:T(8,128)S(1)} %get-tuple-element.656), channel_id=1, source_target_pairs={{0,1},{1,2},{2,3},{3,4},{4,5},{5,6},{6,7},{8,9},{9,10},{10,11},{11... | collective-permute-start | bytes 98312 | tf_op jit(solution)/shard_map/while/body/eval_jaxpr/ppermute | solution.py:19
  104.7 1.6 collective-permute-done.3
  106.5 1.3 collective-permute-start.4
  107.8 5.8 %collective-permute-start.5 = (f32[1,1,32,256]{3,2,1,0:T(8,128)S(1)}, f32[1,1,32,256]{3,2,1,0:T(8,128)S(1)}, u32[]{:S(2)}, u32[]{:S(2)}) collective-permute-start(f32[1,1,32,256]{3,2,1,0:T(8,128)S(1)} %get-tuple-element.658), channel_id=1, source_target_pairs={{0,1},{1,2},{2,3},{3,4},{4,5},{5,6},{6,7},{8,9},{9,10},{10,11},{11... | collective-permute-start | bytes 98312 | tf_op jit(solution)/shard_map/while/body/eval_jaxpr/ppermute | solution.py:19
  113.6 1.6 collective-permute-done.5
  115.8 1.6 constant_dynamic-update-slice_fusion.2
  117.4 1.4 collective-permute-start.6
  118.8 5.8 %collective-permute-start.7 = (f32[2,1,1,32,256]{4,3,2,1,0:T(8,128)S(1)}, f32[2,1,1,32,256]{4,3,2,1,0:T(8,128)S(1)}, u32[]{:S(2)}, u32[]{:S(2)}) collective-permute-start(f32[2,1,1,32,256]{4,3,2,1,0:T(8,128)S(1)} %get-tuple-element.662), channel_id=1, source_target_pairs={{0,1},{1,2},{2,3},{3,4},{4,5},{5,6},{6,7},{8,9},{9,10},{10,11},{11... | collective-permute-start | bytes 196616 | tf_op jit(solution)/shard_map/while/body/eval_jaxpr/ppermute | solution.py:19
  124.7 4.0 %fusion.137 = f32[]{:T(128)} fusion(f32[32]{0:T(128)S(1)} %get-tuple-element.718, f32[32768,1]{0,1:T(1,128)S(1)} %bitcast.144, s32[32768]{0:T(1024)S(1)} %copy-done.6, s32[32]{0:T(128)S(1)} %get-tuple-element.720, f32[1,4,32]{2,1,0:T(4,128)S(1)} %get-tuple-element.717, s32[]{:T(128)S(6)} %copy.28), kind=kOutput, calls=%fused_computation.10.clone.1 | convolution fusion | flops 14680191 | bytes 262536 | tf_op jit(solution)/shard_map/while/body/eval_jaxpr/dot_general | solution.py:148
  131.8 5.9 %collective-permute-start.1 = (f32[2,1,1,32,256]{4,3,2,1,0:T(8,128)S(1)}, f32[2,1,1,32,256]{4,3,2,1,0:T(8,128)S(1)}, u32[]{:S(2)}, u32[]{:S(2)}) collective-permute-start(f32[2,1,1,32,256]{4,3,2,1,0:T(8,128)S(1)} %get-tuple-element.644), channel_id=1, source_target_pairs={{0,1},{1,2},{2,3},{3,4},{4,5},{5,6},{6,7},{8,9},{9,10},{10,11},{11... | collective-permute-start | bytes 196616 | tf_op jit(solution)/shard_map/while/body/eval_jaxpr/ppermute | solution.py:19
  138.1 1.7 collective-permute-done.1
  139.9 1.3 fusion.133
  142.6 5.4 %collective-permute-start.3 = (f32[1,1,32,256]{3,2,1,0:T(8,128)S(1)}, f32[1,1,32,256]{3,2,1,0:T(8,128)S(1)}, u32[]{:S(2)}, u32[]{:S(2)}) collective-permute-start(f32[1,1,32,256]{3,2,1,0:T(8,128)S(1)} %get-tuple-element.656), channel_id=1, source_target_pairs={{0,1},{1,2},{2,3},{3,4},{4,5},{5,6},{6,7},{8,9},{9,10},{10,11},{11... | collective-permute-start | bytes 98312 | tf_op jit(solution)/shard_map/while/body/eval_jaxpr/ppermute | solution.py:19
  148.0 1.6 collective-permute-done.3
  149.7 1.3 collective-permute-start.4
  151.0 5.9 %collective-permute-start.5 = (f32[1,1,32,256]{3,2,1,0:T(8,128)S(1)}, f32[1,1,32,256]{3,2,1,0:T(8,128)S(1)}, u32[]{:S(2)}, u32[]{:S(2)}) collective-permute-start(f32[1,1,32,256]{3,2,1,0:T(8,128)S(1)} %get-tuple-element.658), channel_id=1, source_target_pairs={{0,1},{1,2},{2,3},{3,4},{4,5},{5,6},{6,7},{8,9},{9,10},{10,11},{11... | collective-permute-start | bytes 98312 | tf_op jit(solution)/shard_map/while/body/eval_jaxpr/ppermute | solution.py:19
  157.1 1.5 collective-permute-done.5
  159.2 1.6 constant_dynamic-update-slice_fusion.2
  160.8 1.4 collective-permute-start.6
  162.2 5.7 %collective-permute-start.7 = (f32[2,1,1,32,256]{4,3,2,1,0:T(8,128)S(1)}, f32[2,1,1,32,256]{4,3,2,1,0:T(8,128)S(1)}, u32[]{:S(2)}, u32[]{:S(2)}) collective-permute-start(f32[2,1,1,32,256]{4,3,2,1,0:T(8,128)S(1)} %get-tuple-element.662), channel_id=1, source_target_pairs={{0,1},{1,2},{2,3},{3,4},{4,5},{5,6},{6,7},{8,9},{9,10},{10,11},{11... | collective-permute-start | bytes 196616 | tf_op jit(solution)/shard_map/while/body/eval_jaxpr/ppermute | solution.py:19
  168.1 4.0 %fusion.137 = f32[]{:T(128)} fusion(f32[32]{0:T(128)S(1)} %get-tuple-element.718, f32[32768,1]{0,1:T(1,128)S(1)} %bitcast.144, s32[32768]{0:T(1024)S(1)} %copy-done.6, s32[32]{0:T(128)S(1)} %get-tuple-element.720, f32[1,4,32]{2,1,0:T(4,128)S(1)} %get-tuple-element.717, s32[]{:T(128)S(6)} %copy.28), kind=kOutput, calls=%fused_computation.10.clone.1 | convolution fusion | flops 14680191 | bytes 262536 | tf_op jit(solution)/shard_map/while/body/eval_jaxpr/dot_general | solution.py:148
  175.2 5.8 %collective-permute-start.1 = (f32[2,1,1,32,256]{4,3,2,1,0:T(8,128)S(1)}, f32[2,1,1,32,256]{4,3,2,1,0:T(8,128)S(1)}, u32[]{:S(2)}, u32[]{:S(2)}) collective-permute-start(f32[2,1,1,32,256]{4,3,2,1,0:T(8,128)S(1)} %get-tuple-element.644), channel_id=1, source_target_pairs={{0,1},{1,2},{2,3},{3,4},{4,5},{5,6},{6,7},{8,9},{9,10},{10,11},{11... | collective-permute-start | bytes 196616 | tf_op jit(solution)/shard_map/while/body/eval_jaxpr/ppermute | solution.py:19
  181.3 1.6 collective-permute-done.1
  183.0 1.3 fusion.133
  185.6 5.4 %collective-permute-start.3 = (f32[1,1,32,256]{3,2,1,0:T(8,128)S(1)}, f32[1,1,32,256]{3,2,1,0:T(8,128)S(1)}, u32[]{:S(2)}, u32[]{:S(2)}) collective-permute-start(f32[1,1,32,256]{3,2,1,0:T(8,128)S(1)} %get-tuple-element.656), channel_id=1, source_target_pairs={{0,1},{1,2},{2,3},{3,4},{4,5},{5,6},{6,7},{8,9},{9,10},{10,11},{11... | collective-permute-start | bytes 98312 | tf_op jit(solution)/shard_map/while/body/eval_jaxpr/ppermute | solution.py:19
  191.0 1.6 collective-permute-done.3
  192.8 1.3 collective-permute-start.4
  194.1 5.8 %collective-permute-start.5 = (f32[1,1,32,256]{3,2,1,0:T(8,128)S(1)}, f32[1,1,32,256]{3,2,1,0:T(8,128)S(1)}, u32[]{:S(2)}, u32[]{:S(2)}) collective-permute-start(f32[1,1,32,256]{3,2,1,0:T(8,128)S(1)} %get-tuple-element.658), channel_id=1, source_target_pairs={{0,1},{1,2},{2,3},{3,4},{4,5},{5,6},{6,7},{8,9},{9,10},{10,11},{11... | collective-permute-start | bytes 98312 | tf_op jit(solution)/shard_map/while/body/eval_jaxpr/ppermute | solution.py:19
  199.9 1.6 collective-permute-done.5
  202.1 1.6 constant_dynamic-update-slice_fusion.2
  203.7 1.4 collective-permute-start.6
  205.1 5.8 %collective-permute-start.7 = (f32[2,1,1,32,256]{4,3,2,1,0:T(8,128)S(1)}, f32[2,1,1,32,256]{4,3,2,1,0:T(8,128)S(1)}, u32[]{:S(2)}, u32[]{:S(2)}) collective-permute-start(f32[2,1,1,32,256]{4,3,2,1,0:T(8,128)S(1)} %get-tuple-element.662), channel_id=1, source_target_pairs={{0,1},{1,2},{2,3},{3,4},{4,5},{5,6},{6,7},{8,9},{9,10},{10,11},{11... | collective-permute-start | bytes 196616 | tf_op jit(solution)/shard_map/while/body/eval_jaxpr/ppermute | solution.py:19
  211.0 4.0 %fusion.137 = f32[]{:T(128)} fusion(f32[32]{0:T(128)S(1)} %get-tuple-element.718, f32[32768,1]{0,1:T(1,128)S(1)} %bitcast.144, s32[32768]{0:T(1024)S(1)} %copy-done.6, s32[32]{0:T(128)S(1)} %get-tuple-element.720, f32[1,4,32]{2,1,0:T(4,128)S(1)} %get-tuple-element.717, s32[]{:T(128)S(6)} %copy.28), kind=kOutput, calls=%fused_computation.10.clone.1 | convolution fusion | flops 14680191 | bytes 262536 | tf_op jit(solution)/shard_map/while/body/eval_jaxpr/dot_general | solution.py:148
  216.8 12.3 %all_to_all.36 = f32[4,1,4,32,256]{4,3,2,1,0:T(8,128)S(1)} all-to-all(f32[4,1,4,32,256]{4,3,2,1,0:T(8,128)} %get-tuple-element.380), channel_id=1, replica_groups=mesh['tm'=4,'space'=8] {'tm'}, dimensions={0} | all-to-all | bytes 1048576 | tf_op jit(solution)/shard_map/all_to_all | solution.py:189
  229.0 3.5 %all-to-all-start.2 = ((f32[4,1,4,32,256]{4,3,2,1,0:T(8,128)}), f32[4,1,4,32,256]{4,3,2,1,0:T(8,128)S(1)}, u32[]{:S(2)}, u32[]{:S(2)}) async-start(f32[4,1,4,32,256]{4,3,2,1,0:T(8,128)} %get-tuple-element.381), calls=%async_computation.2 | async-start | bytes 1048576 | tf_op jit(solution)/shard_map/all_to_all | solution.py:190
  232.6 46.4 %psum.7 = f32[4]{0:T(128)S(1)} all-reduce(f32[4]{0:T(128)S(1)} %dynamic_update_slice.24), channel_id=1, replica_groups=mesh['tm'=4,'space'=8] {'tm','space'}, use_global_device_ids=true, to_apply=%region_4.5 | all-reduce | flops 4 | bytes 32 | tf_op jit(solution)/shard_map/psum | solution.py:193
  (149 shorter events, 20.7 us)
Async XLA Ops:
  0.6 28.9 %copy-start = (f32[4,4,32,256]{3,2,1,0:T(8,128)S(1)}, f32[4,4,32,256]{3,2,1,0:T(8,128)}, u32[]{:S(2)}) copy-start(f32[4,4,32,256]{3,2,1,0:T(8,128)} %param.12) | copy-start | bytes 1572868
  0.6 4.4 %copy-start.10 = (f32[3,8]{1,0:T(4,128)S(1)}, f32[3,8]{1,0:T(4,128)}, u32[]{:S(2)}) copy-start(f32[3,8]{1,0:T(4,128)} %param.18) | copy-start | bytes 292
  0.7 11.2 %copy-start.11 = (s32[32]{0:T(128)S(1)}, s32[32]{0:T(128)}, u32[]{:S(2)}) copy-start(s32[32]{0:T(128)} %param.19) | copy-start | bytes 388
  0.7 6.0 %copy-start.12 = (f32[1,32]{1,0:T(1,128)S(1)}, f32[1,32]{1,0:T(1,128)}, u32[]{:S(2)}) copy-start(f32[1,32]{1,0:T(1,128)} %param.20) | copy-start | bytes 388
  0.7 44.4 %all-to-all-start = ((f32[4,1,32]{2,1,0:T(1,128)}), f32[4,1,32]{2,1,0:T(1,128)S(1)}, u32[]{:S(2)}, u32[]{:S(2)}) async-start(f32[4,1,32]{2,1,0:T(1,128)} %param.21), calls=%async_computation | async-start | bytes 4096 | tf_op jit(solution)/shard_map/all_to_all | solution.py:159
  6.6 7.3 %copy-start.5 = (s32[16,2,8,128]{3,1,2,0:T(2,128)}, s32[16,2,8,128]{3,1,2,0:T(2,128)S(1)}, u32[]{:S(2)}) copy-start(s32[16,2,8,128]{3,1,2,0:T(2,128)S(1)} %copy.16) | copy-start | bytes 393220
  12.6 1.4 copy-start.7
  13.9 8.2 %copy-start.8 = (f32[1,4,32,256]{3,2,1,0:T(8,128)S(1)}, f32[1,4,32,256]{3,2,1,0:T(8,128)}, u32[]{:S(2)}) copy-start(f32[1,4,32,256]{3,2,1,0:T(8,128)} %param.13) | copy-start | bytes 393220
  22.1 7.4 %copy-start.9 = (s32[4,32,256]{2,1,0:T(8,128)S(1)}, s32[4,32,256]{2,1,0:T(8,128)}, u32[]{:S(2)}) copy-start(s32[4,32,256]{2,1,0:T(8,128)} %param.17) | copy-start | bytes 393220
  45.0 0.9 copy-start.1
  45.0 1.0 copy-start.2
  46.0 6.4 %collective-permute-start = (f32[2,1,1,32,256]{4,3,2,1,0:T(8,128)S(1)}, f32[2,1,1,32,256]{4,3,2,1,0:T(8,128)S(1)}, u32[]{:S(2)}, u32[]{:S(2)}) collective-permute-start(f32[2,1,1,32,256]{4,3,2,1,0:T(8,128)S(1)} %get-tuple-element.643), channel_id=1, source_target_pairs={{1,0},{2,1},{3,2},{4,3},{5,4},{6,5},{7,6},{9,8},{10,9},{11,10},{12... | collective-permute-start | bytes 196616 | tf_op jit(solution)/shard_map/while/body/eval_jaxpr/ppermute | solution.py:21
  47.3 6.7 %collective-permute-start.1 = (f32[2,1,1,32,256]{4,3,2,1,0:T(8,128)S(1)}, f32[2,1,1,32,256]{4,3,2,1,0:T(8,128)S(1)}, u32[]{:S(2)}, u32[]{:S(2)}) collective-permute-start(f32[2,1,1,32,256]{4,3,2,1,0:T(8,128)S(1)} %get-tuple-element.644), channel_id=1, source_target_pairs={{0,1},{1,2},{2,3},{3,4},{4,5},{5,6},{6,7},{8,9},{9,10},{10,11},{11... | collective-permute-start | bytes 196616 | tf_op jit(solution)/shard_map/while/body/eval_jaxpr/ppermute | solution.py:19
  55.4 6.4 %collective-permute-start.2 = (f32[1,1,32,256]{3,2,1,0:T(8,128)S(1)}, f32[1,1,32,256]{3,2,1,0:T(8,128)S(1)}, u32[]{:S(2)}, u32[]{:S(2)}) collective-permute-start(f32[1,1,32,256]{3,2,1,0:T(8,128)S(1)} %get-tuple-element.655), channel_id=1, source_target_pairs={{1,0},{2,1},{3,2},{4,3},{5,4},{6,5},{7,6},{9,8},{10,9},{11,10},{12... | collective-permute-start | bytes 98312 | tf_op jit(solution)/shard_map/while/body/eval_jaxpr/ppermute | solution.py:21
  56.7 6.7 %collective-permute-start.3 = (f32[1,1,32,256]{3,2,1,0:T(8,128)S(1)}, f32[1,1,32,256]{3,2,1,0:T(8,128)S(1)}, u32[]{:S(2)}, u32[]{:S(2)}) collective-permute-start(f32[1,1,32,256]{3,2,1,0:T(8,128)S(1)} %get-tuple-element.656), channel_id=1, source_target_pairs={{0,1},{1,2},{2,3},{3,4},{4,5},{5,6},{6,7},{8,9},{9,10},{10,11},{11... | collective-permute-start | bytes 98312 | tf_op jit(solution)/shard_map/while/body/eval_jaxpr/ppermute | solution.py:19
  63.6 7.1 %collective-permute-start.4 = (f32[1,1,32,256]{3,2,1,0:T(8,128)S(1)}, f32[1,1,32,256]{3,2,1,0:T(8,128)S(1)}, u32[]{:S(2)}, u32[]{:S(2)}) collective-permute-start(f32[1,1,32,256]{3,2,1,0:T(8,128)S(1)} %get-tuple-element.657), channel_id=1, source_target_pairs={{1,0},{2,1},{3,2},{4,3},{5,4},{6,5},{7,6},{9,8},{10,9},{11,10},{12... | collective-permute-start | bytes 98312 | tf_op jit(solution)/shard_map/while/body/eval_jaxpr/ppermute | solution.py:21
  64.9 7.4 %collective-permute-start.5 = (f32[1,1,32,256]{3,2,1,0:T(8,128)S(1)}, f32[1,1,32,256]{3,2,1,0:T(8,128)S(1)}, u32[]{:S(2)}, u32[]{:S(2)}) collective-permute-start(f32[1,1,32,256]{3,2,1,0:T(8,128)S(1)} %get-tuple-element.658), channel_id=1, source_target_pairs={{0,1},{1,2},{2,3},{3,4},{4,5},{5,6},{6,7},{8,9},{9,10},{10,11},{11... | collective-permute-start | bytes 98312 | tf_op jit(solution)/shard_map/while/body/eval_jaxpr/ppermute | solution.py:19
  70.7 1.6 copy-start.3
  72.3 0.6 copy-start.4
  74.4 7.4 %copy-start.6 = (s32[32768]{0:T(1024)S(1)}, s32[32768]{0:T(1024)}, u32[]{:S(2)}) copy-start(s32[32768]{0:T(1024)} %get-tuple-element.719) | copy-start | bytes 393220 | tf_op jit(solution)/shard_map/while
  74.4 12.0 %collective-permute-start.6 = (f32[2,1,1,32,256]{4,3,2,1,0:T(8,128)S(1)}, f32[2,1,1,32,256]{4,3,2,1,0:T(8,128)S(1)}, u32[]{:S(2)}, u32[]{:S(2)}) collective-permute-start(f32[2,1,1,32,256]{4,3,2,1,0:T(8,128)S(1)} %get-tuple-element.661), channel_id=1, source_target_pairs={{1,0},{2,1},{3,2},{4,3},{5,4},{6,5},{7,6},{9,8},{10,9},{11,10},{12... | collective-permute-start | bytes 196616 | tf_op jit(solution)/shard_map/while/body/eval_jaxpr/ppermute | solution.py:21
  75.9 10.6 %collective-permute-start.7 = (f32[2,1,1,32,256]{4,3,2,1,0:T(8,128)S(1)}, f32[2,1,1,32,256]{4,3,2,1,0:T(8,128)S(1)}, u32[]{:S(2)}, u32[]{:S(2)}) collective-permute-start(f32[2,1,1,32,256]{4,3,2,1,0:T(8,128)S(1)} %get-tuple-element.662), channel_id=1, source_target_pairs={{0,1},{1,2},{2,3},{3,4},{4,5},{5,6},{6,7},{8,9},{9,10},{10,11},{11... | collective-permute-start | bytes 196616 | tf_op jit(solution)/shard_map/while/body/eval_jaxpr/ppermute | solution.py:19
  87.6 7.4 %collective-permute-start = (f32[2,1,1,32,256]{4,3,2,1,0:T(8,128)S(1)}, f32[2,1,1,32,256]{4,3,2,1,0:T(8,128)S(1)}, u32[]{:S(2)}, u32[]{:S(2)}) collective-permute-start(f32[2,1,1,32,256]{4,3,2,1,0:T(8,128)S(1)} %get-tuple-element.643), channel_id=1, source_target_pairs={{1,0},{2,1},{3,2},{4,3},{5,4},{6,5},{7,6},{9,8},{10,9},{11,10},{12... | collective-permute-start | bytes 196616 | tf_op jit(solution)/shard_map/while/body/eval_jaxpr/ppermute | solution.py:21
  88.9 7.6 %collective-permute-start.1 = (f32[2,1,1,32,256]{4,3,2,1,0:T(8,128)S(1)}, f32[2,1,1,32,256]{4,3,2,1,0:T(8,128)S(1)}, u32[]{:S(2)}, u32[]{:S(2)}) collective-permute-start(f32[2,1,1,32,256]{4,3,2,1,0:T(8,128)S(1)} %get-tuple-element.644), channel_id=1, source_target_pairs={{0,1},{1,2},{2,3},{3,4},{4,5},{5,6},{6,7},{8,9},{9,10},{10,11},{11... | collective-permute-start | bytes 196616 | tf_op jit(solution)/shard_map/while/body/eval_jaxpr/ppermute | solution.py:19
  98.0 6.8 %collective-permute-start.2 = (f32[1,1,32,256]{3,2,1,0:T(8,128)S(1)}, f32[1,1,32,256]{3,2,1,0:T(8,128)S(1)}, u32[]{:S(2)}, u32[]{:S(2)}) collective-permute-start(f32[1,1,32,256]{3,2,1,0:T(8,128)S(1)} %get-tuple-element.655), channel_id=1, source_target_pairs={{1,0},{2,1},{3,2},{4,3},{5,4},{6,5},{7,6},{9,8},{10,9},{11,10},{12... | collective-permute-start | bytes 98312 | tf_op jit(solution)/shard_map/while/body/eval_jaxpr/ppermute | solution.py:21
  99.3 7.0 %collective-permute-start.3 = (f32[1,1,32,256]{3,2,1,0:T(8,128)S(1)}, f32[1,1,32,256]{3,2,1,0:T(8,128)S(1)}, u32[]{:S(2)}, u32[]{:S(2)}) collective-permute-start(f32[1,1,32,256]{3,2,1,0:T(8,128)S(1)} %get-tuple-element.656), channel_id=1, source_target_pairs={{0,1},{1,2},{2,3},{3,4},{4,5},{5,6},{6,7},{8,9},{9,10},{10,11},{11... | collective-permute-start | bytes 98312 | tf_op jit(solution)/shard_map/while/body/eval_jaxpr/ppermute | solution.py:19
  106.5 7.1 %collective-permute-start.4 = (f32[1,1,32,256]{3,2,1,0:T(8,128)S(1)}, f32[1,1,32,256]{3,2,1,0:T(8,128)S(1)}, u32[]{:S(2)}, u32[]{:S(2)}) collective-permute-start(f32[1,1,32,256]{3,2,1,0:T(8,128)S(1)} %get-tuple-element.657), channel_id=1, source_target_pairs={{1,0},{2,1},{3,2},{4,3},{5,4},{6,5},{7,6},{9,8},{10,9},{11,10},{12... | collective-permute-start | bytes 98312 | tf_op jit(solution)/shard_map/while/body/eval_jaxpr/ppermute | solution.py:21
  107.8 7.4 %collective-permute-start.5 = (f32[1,1,32,256]{3,2,1,0:T(8,128)S(1)}, f32[1,1,32,256]{3,2,1,0:T(8,128)S(1)}, u32[]{:S(2)}, u32[]{:S(2)}) collective-permute-start(f32[1,1,32,256]{3,2,1,0:T(8,128)S(1)} %get-tuple-element.658), channel_id=1, source_target_pairs={{0,1},{1,2},{2,3},{3,4},{4,5},{5,6},{6,7},{8,9},{9,10},{10,11},{11... | collective-permute-start | bytes 98312 | tf_op jit(solution)/shard_map/while/body/eval_jaxpr/ppermute | solution.py:19
  113.6 1.6 copy-start.3
  115.2 0.6 copy-start.4
  117.3 7.4 %copy-start.6 = (s32[32768]{0:T(1024)S(1)}, s32[32768]{0:T(1024)}, u32[]{:S(2)}) copy-start(s32[32768]{0:T(1024)} %get-tuple-element.719) | copy-start | bytes 393220 | tf_op jit(solution)/shard_map/while
  117.4 12.0 %collective-permute-start.6 = (f32[2,1,1,32,256]{4,3,2,1,0:T(8,128)S(1)}, f32[2,1,1,32,256]{4,3,2,1,0:T(8,128)S(1)}, u32[]{:S(2)}, u32[]{:S(2)}) collective-permute-start(f32[2,1,1,32,256]{4,3,2,1,0:T(8,128)S(1)} %get-tuple-element.661), channel_id=1, source_target_pairs={{1,0},{2,1},{3,2},{4,3},{5,4},{6,5},{7,6},{9,8},{10,9},{11,10},{12... | collective-permute-start | bytes 196616 | tf_op jit(solution)/shard_map/while/body/eval_jaxpr/ppermute | solution.py:21
  118.8 10.6 %collective-permute-start.7 = (f32[2,1,1,32,256]{4,3,2,1,0:T(8,128)S(1)}, f32[2,1,1,32,256]{4,3,2,1,0:T(8,128)S(1)}, u32[]{:S(2)}, u32[]{:S(2)}) collective-permute-start(f32[2,1,1,32,256]{4,3,2,1,0:T(8,128)S(1)} %get-tuple-element.662), channel_id=1, source_target_pairs={{0,1},{1,2},{2,3},{3,4},{4,5},{5,6},{6,7},{8,9},{9,10},{10,11},{11... | collective-permute-start | bytes 196616 | tf_op jit(solution)/shard_map/while/body/eval_jaxpr/ppermute | solution.py:19
  130.5 7.6 %collective-permute-start = (f32[2,1,1,32,256]{4,3,2,1,0:T(8,128)S(1)}, f32[2,1,1,32,256]{4,3,2,1,0:T(8,128)S(1)}, u32[]{:S(2)}, u32[]{:S(2)}) collective-permute-start(f32[2,1,1,32,256]{4,3,2,1,0:T(8,128)S(1)} %get-tuple-element.643), channel_id=1, source_target_pairs={{1,0},{2,1},{3,2},{4,3},{5,4},{6,5},{7,6},{9,8},{10,9},{11,10},{12... | collective-permute-start | bytes 196616 | tf_op jit(solution)/shard_map/while/body/eval_jaxpr/ppermute | solution.py:21
  131.8 8.0 %collective-permute-start.1 = (f32[2,1,1,32,256]{4,3,2,1,0:T(8,128)S(1)}, f32[2,1,1,32,256]{4,3,2,1,0:T(8,128)S(1)}, u32[]{:S(2)}, u32[]{:S(2)}) collective-permute-start(f32[2,1,1,32,256]{4,3,2,1,0:T(8,128)S(1)} %get-tuple-element.644), channel_id=1, source_target_pairs={{0,1},{1,2},{2,3},{3,4},{4,5},{5,6},{6,7},{8,9},{9,10},{10,11},{11... | collective-permute-start | bytes 196616 | tf_op jit(solution)/shard_map/while/body/eval_jaxpr/ppermute | solution.py:19
  141.3 6.7 %collective-permute-start.2 = (f32[1,1,32,256]{3,2,1,0:T(8,128)S(1)}, f32[1,1,32,256]{3,2,1,0:T(8,128)S(1)}, u32[]{:S(2)}, u32[]{:S(2)}) collective-permute-start(f32[1,1,32,256]{3,2,1,0:T(8,128)S(1)} %get-tuple-element.655), channel_id=1, source_target_pairs={{1,0},{2,1},{3,2},{4,3},{5,4},{6,5},{7,6},{9,8},{10,9},{11,10},{12... | collective-permute-start | bytes 98312 | tf_op jit(solution)/shard_map/while/body/eval_jaxpr/ppermute | solution.py:21
  142.6 7.0 %collective-permute-start.3 = (f32[1,1,32,256]{3,2,1,0:T(8,128)S(1)}, f32[1,1,32,256]{3,2,1,0:T(8,128)S(1)}, u32[]{:S(2)}, u32[]{:S(2)}) collective-permute-start(f32[1,1,32,256]{3,2,1,0:T(8,128)S(1)} %get-tuple-element.656), channel_id=1, source_target_pairs={{0,1},{1,2},{2,3},{3,4},{4,5},{5,6},{6,7},{8,9},{9,10},{10,11},{11... | collective-permute-start | bytes 98312 | tf_op jit(solution)/shard_map/while/body/eval_jaxpr/ppermute | solution.py:19
  149.7 7.3 %collective-permute-start.4 = (f32[1,1,32,256]{3,2,1,0:T(8,128)S(1)}, f32[1,1,32,256]{3,2,1,0:T(8,128)S(1)}, u32[]{:S(2)}, u32[]{:S(2)}) collective-permute-start(f32[1,1,32,256]{3,2,1,0:T(8,128)S(1)} %get-tuple-element.657), channel_id=1, source_target_pairs={{1,0},{2,1},{3,2},{4,3},{5,4},{6,5},{7,6},{9,8},{10,9},{11,10},{12... | collective-permute-start | bytes 98312 | tf_op jit(solution)/shard_map/while/body/eval_jaxpr/ppermute | solution.py:21
  151.0 7.6 %collective-permute-start.5 = (f32[1,1,32,256]{3,2,1,0:T(8,128)S(1)}, f32[1,1,32,256]{3,2,1,0:T(8,128)S(1)}, u32[]{:S(2)}, u32[]{:S(2)}) collective-permute-start(f32[1,1,32,256]{3,2,1,0:T(8,128)S(1)} %get-tuple-element.658), channel_id=1, source_target_pairs={{0,1},{1,2},{2,3},{3,4},{4,5},{5,6},{6,7},{8,9},{9,10},{10,11},{11... | collective-permute-start | bytes 98312 | tf_op jit(solution)/shard_map/while/body/eval_jaxpr/ppermute | solution.py:19
  157.1 1.5 copy-start.3
  158.6 0.6 copy-start.4
  160.8 7.3 %copy-start.6 = (s32[32768]{0:T(1024)S(1)}, s32[32768]{0:T(1024)}, u32[]{:S(2)}) copy-start(s32[32768]{0:T(1024)} %get-tuple-element.719) | copy-start | bytes 393220 | tf_op jit(solution)/shard_map/while
  160.8 12.0 %collective-permute-start.6 = (f32[2,1,1,32,256]{4,3,2,1,0:T(8,128)S(1)}, f32[2,1,1,32,256]{4,3,2,1,0:T(8,128)S(1)}, u32[]{:S(2)}, u32[]{:S(2)}) collective-permute-start(f32[2,1,1,32,256]{4,3,2,1,0:T(8,128)S(1)} %get-tuple-element.661), channel_id=1, source_target_pairs={{1,0},{2,1},{3,2},{4,3},{5,4},{6,5},{7,6},{9,8},{10,9},{11,10},{12... | collective-permute-start | bytes 196616 | tf_op jit(solution)/shard_map/while/body/eval_jaxpr/ppermute | solution.py:21
  162.2 10.5 %collective-permute-start.7 = (f32[2,1,1,32,256]{4,3,2,1,0:T(8,128)S(1)}, f32[2,1,1,32,256]{4,3,2,1,0:T(8,128)S(1)}, u32[]{:S(2)}, u32[]{:S(2)}) collective-permute-start(f32[2,1,1,32,256]{4,3,2,1,0:T(8,128)S(1)} %get-tuple-element.662), channel_id=1, source_target_pairs={{0,1},{1,2},{2,3},{3,4},{4,5},{5,6},{6,7},{8,9},{9,10},{10,11},{11... | collective-permute-start | bytes 196616 | tf_op jit(solution)/shard_map/while/body/eval_jaxpr/ppermute | solution.py:19
  173.9 7.4 %collective-permute-start = (f32[2,1,1,32,256]{4,3,2,1,0:T(8,128)S(1)}, f32[2,1,1,32,256]{4,3,2,1,0:T(8,128)S(1)}, u32[]{:S(2)}, u32[]{:S(2)}) collective-permute-start(f32[2,1,1,32,256]{4,3,2,1,0:T(8,128)S(1)} %get-tuple-element.643), channel_id=1, source_target_pairs={{1,0},{2,1},{3,2},{4,3},{5,4},{6,5},{7,6},{9,8},{10,9},{11,10},{12... | collective-permute-start | bytes 196616 | tf_op jit(solution)/shard_map/while/body/eval_jaxpr/ppermute | solution.py:21
  175.2 7.6 %collective-permute-start.1 = (f32[2,1,1,32,256]{4,3,2,1,0:T(8,128)S(1)}, f32[2,1,1,32,256]{4,3,2,1,0:T(8,128)S(1)}, u32[]{:S(2)}, u32[]{:S(2)}) collective-permute-start(f32[2,1,1,32,256]{4,3,2,1,0:T(8,128)S(1)} %get-tuple-element.644), channel_id=1, source_target_pairs={{0,1},{1,2},{2,3},{3,4},{4,5},{5,6},{6,7},{8,9},{9,10},{10,11},{11... | collective-permute-start | bytes 196616 | tf_op jit(solution)/shard_map/while/body/eval_jaxpr/ppermute | solution.py:19
  184.3 6.8 %collective-permute-start.2 = (f32[1,1,32,256]{3,2,1,0:T(8,128)S(1)}, f32[1,1,32,256]{3,2,1,0:T(8,128)S(1)}, u32[]{:S(2)}, u32[]{:S(2)}) collective-permute-start(f32[1,1,32,256]{3,2,1,0:T(8,128)S(1)} %get-tuple-element.655), channel_id=1, source_target_pairs={{1,0},{2,1},{3,2},{4,3},{5,4},{6,5},{7,6},{9,8},{10,9},{11,10},{12... | collective-permute-start | bytes 98312 | tf_op jit(solution)/shard_map/while/body/eval_jaxpr/ppermute | solution.py:21
  185.6 7.0 %collective-permute-start.3 = (f32[1,1,32,256]{3,2,1,0:T(8,128)S(1)}, f32[1,1,32,256]{3,2,1,0:T(8,128)S(1)}, u32[]{:S(2)}, u32[]{:S(2)}) collective-permute-start(f32[1,1,32,256]{3,2,1,0:T(8,128)S(1)} %get-tuple-element.656), channel_id=1, source_target_pairs={{0,1},{1,2},{2,3},{3,4},{4,5},{5,6},{6,7},{8,9},{9,10},{10,11},{11... | collective-permute-start | bytes 98312 | tf_op jit(solution)/shard_map/while/body/eval_jaxpr/ppermute | solution.py:19
  192.8 7.1 %collective-permute-start.4 = (f32[1,1,32,256]{3,2,1,0:T(8,128)S(1)}, f32[1,1,32,256]{3,2,1,0:T(8,128)S(1)}, u32[]{:S(2)}, u32[]{:S(2)}) collective-permute-start(f32[1,1,32,256]{3,2,1,0:T(8,128)S(1)} %get-tuple-element.657), channel_id=1, source_target_pairs={{1,0},{2,1},{3,2},{4,3},{5,4},{6,5},{7,6},{9,8},{10,9},{11,10},{12... | collective-permute-start | bytes 98312 | tf_op jit(solution)/shard_map/while/body/eval_jaxpr/ppermute | solution.py:21
  194.1 7.4 %collective-permute-start.5 = (f32[1,1,32,256]{3,2,1,0:T(8,128)S(1)}, f32[1,1,32,256]{3,2,1,0:T(8,128)S(1)}, u32[]{:S(2)}, u32[]{:S(2)}) collective-permute-start(f32[1,1,32,256]{3,2,1,0:T(8,128)S(1)} %get-tuple-element.658), channel_id=1, source_target_pairs={{0,1},{1,2},{2,3},{3,4},{4,5},{5,6},{6,7},{8,9},{9,10},{10,11},{11... | collective-permute-start | bytes 98312 | tf_op jit(solution)/shard_map/while/body/eval_jaxpr/ppermute | solution.py:19
  199.9 1.6 copy-start.3
  201.5 0.6 copy-start.4
  203.6 7.4 %copy-start.6 = (s32[32768]{0:T(1024)S(1)}, s32[32768]{0:T(1024)}, u32[]{:S(2)}) copy-start(s32[32768]{0:T(1024)} %get-tuple-element.719) | copy-start | bytes 393220 | tf_op jit(solution)/shard_map/while
  203.7 12.0 %collective-permute-start.6 = (f32[2,1,1,32,256]{4,3,2,1,0:T(8,128)S(1)}, f32[2,1,1,32,256]{4,3,2,1,0:T(8,128)S(1)}, u32[]{:S(2)}, u32[]{:S(2)}) collective-permute-start(f32[2,1,1,32,256]{4,3,2,1,0:T(8,128)S(1)} %get-tuple-element.661), channel_id=1, source_target_pairs={{1,0},{2,1},{3,2},{4,3},{5,4},{6,5},{7,6},{9,8},{10,9},{11,10},{12... | collective-permute-start | bytes 196616 | tf_op jit(solution)/shard_map/while/body/eval_jaxpr/ppermute | solution.py:21
  205.1 10.6 %collective-permute-start.7 = (f32[2,1,1,32,256]{4,3,2,1,0:T(8,128)S(1)}, f32[2,1,1,32,256]{4,3,2,1,0:T(8,128)S(1)}, u32[]{:S(2)}, u32[]{:S(2)}) collective-permute-start(f32[2,1,1,32,256]{4,3,2,1,0:T(8,128)S(1)} %get-tuple-element.662), channel_id=1, source_target_pairs={{0,1},{1,2},{2,3},{3,4},{4,5},{5,6},{6,7},{8,9},{9,10},{10,11},{11... | collective-permute-start | bytes 196616 | tf_op jit(solution)/shard_map/while/body/eval_jaxpr/ppermute | solution.py:19
  229.0 50.5 %all-to-all-start.2 = ((f32[4,1,4,32,256]{4,3,2,1,0:T(8,128)}), f32[4,1,4,32,256]{4,3,2,1,0:T(8,128)S(1)}, u32[]{:S(2)}, u32[]{:S(2)}) async-start(f32[4,1,4,32,256]{4,3,2,1,0:T(8,128)} %get-tuple-element.381), calls=%async_computation.2 | async-start | bytes 1048576 | tf_op jit(solution)/shard_map/all_to_all | solution.py:190
where the time goes:
time: 283 us; the launch traced here: 281 us
  starting transfers between devices  119 us (42%)
  blocking collectives  79.4 us (28%)
  other arithmetic  33.1 us (12%)
  waiting for transfers between devices  20.6 us (7%)
  matrix products  17.5 us (6%)
  local copies, waits for them, and re-layouts  7.58 us (3%)
  loops' own time  3.42 us (1%)
    ppermute x16, starting transfers between devices, padded(): lax.ppermute(tail, axis, [(i, (i + 1) % count) for i in range(ends)])  89.6 us
    psum x1, blocking collectives, body(): totals = lax.psum(misfit, ('tm', 'space'))  46.4 us
    ppermute x16, starting transfers between devices, padded(): lax.ppermute(head, axis, [((i + 1) % count, i) for i in range(ends)])  21.2 us
    ppermute x16, waiting for transfers between devices, padded(): lax.ppermute(tail, axis, [(i, (i + 1) % count) for i in range(ends)])  18.9 us
    dot_general x4, matrix products, mismatch(): jnp.dot(pressure.reshape(batch_size, -1), well_picks.T, precision=lax.Pre...  16.2 us
    all_to_all x1, blocking collectives, body(): lax.all_to_all(result[2], 'tm', split_axis=0, concat_axis=1, tiled=True)  12.3 us
    add x2, other arithmetic, region_fields(): summed + jnp.where(region_ids == region_index, region_table[table_row, re...  10.3 us
    all_gather x1, blocking collectives, body(): lax.all_gather(inflow, 'tm', axis=0, tiled=True)  8.19 us
  transfers between devices with their start and end apart: 34, of which 17 were waited for; matrix products, arithmetic and copies ran while one was open for 13% of the time, Pallas kernels for 0%

commit v1 on v0

v1 whole, which is shorter than its diff:
```python
import functools

import jax
import jax.numpy as jnp
from jax import lax
from jax.experimental import pallas as pl
from jax.experimental.pallas import tpu as pltpu
from jax.sharding import PartitionSpec as P

ITERS = 3
MESH = pl.DeviceIdType.MESH
EXACT = lax.Precision.HIGHEST


def before(v, axis):
    return pltpu.roll(v, 1, axis)


def after(v, axis):
    return pltpu.roll(v, v.shape[axis] - 1, axis)


def kernel(
    T, N,
    perm, mult, infl, p0, s0, ids, table, small, rows_row,
    mis, outp, outs,
    M, I, SM, MH, PH, HP, HF, PB, SB, FE, TX, TZP, TZM, TYP, TYM, RC, C, V, G, B, Q, E0, E1, E2, ES,
    sM, rM, sI, rI, sS, rS, sMH, rMH, sPH, rPH, sHP, rHP, sHF, rHF, sO, rO, lO, s1, r1, s2, r2,
):
    t = lax.axis_index("tm")
    i = lax.axis_index("space")
    X, Z, Y = p0.shape
    R = T
    W = small.shape[0]
    K = R * ITERS
    has = (i > 0, i < N - 1)
    beside = (i - 1, i + 1)
    edge = (0, X - 1)
    order = [0, X - 1] + list(range(1, X - 1))

    def rdma(src, dst, ss, rs, dev):
        return pltpu.make_async_remote_copy(
            src_ref=src, dst_ref=dst, send_sem=ss, recv_sem=rs, device_id=dev, device_id_type=MESH
        )

    def halo(side, src, dst_slots, ss, rs, peer=None):
        return rdma(
            src, dst_slots.at[1 - side], ss.at[side], rs.at[1 - side],
            (t if peer is None else peer, beside[side]),
        )

    def send_edge(side, src, slots, ss, rs, peer=None):
        @pl.when(has[side])
        def _():
            halo(side, src, slots, ss, rs, peer).start()

    def edge_sent(side, src, slots, ss, rs, peer=None):
        @pl.when(has[side])
        def _():
            halo(side, src, slots, ss, rs, peer).wait_send()

    def edge_here(side, slots, ss, rs):
        @pl.when(has[side])
        def _():
            rdma(slots.at[side], slots.at[side], ss.at[side], rs.at[side], (t, beside[side])).wait_recv()

    def peers():
        return [(d, lax.rem(t + d, T)) for d in range(1, T)]

    for side in (0, 1):
        send_edge(side, p0.at[edge[side]], HP.at[0], sHP.at[0], rHP.at[0])
        send_edge(side, perm.at[t, edge[side]], PH, sPH, rPH)
        send_edge(side, mult.at[0, edge[side]], MH.at[t], sMH.at[0], rMH.at[t])
    for d, peer in peers():
        rdma(small, SM.at[t], sS.at[d], rS.at[t], (peer, i)).start()
        rdma(mult.at[0], M.at[t], sM.at[d], rM.at[t], (peer, i)).start()
        for side in (0, 1):
            send_edge(side, mult.at[0, edge[side]], MH.at[t], sMH.at[d], rMH.at[t], peer)
    for d, peer in peers():
        rdma(infl.at[0], I.at[t], sI.at[d], rI.at[t], (peer, i)).start()

    for side in (0, 1):
        @pl.when(jnp.logical_not(has[side]))
        def _():
            zero = jnp.zeros((Z, Y), jnp.float32)
            PH[side] = zero

            def clear(n, c):
                HP[n, side] = zero
                return c

            lax.fori_loop(0, K + 1, clear, 0)

            def clear_r(n, c):
                HF[n, side] = zero
                MH[n, side] = zero
                return c

            lax.fori_loop(0, R, clear_r, 0)

    M[t] = mult[0]
    I[t] = infl[0]
    SM[t] = small[...]
    PB[0] = p0[...]
    SB[0] = s0[...]

    def fraction(s, v):
        sq = s * s
        rest = (1.0 - s) * (1.0 - s)
        return sq / (sq + v * rest)

    for x in order:
        rock = ids[x]
        c = jnp.zeros((Z, Y), jnp.float32)
        v = c
        g = c
        for k in range(table.shape[1]):
            hit = rock == k
            c = jnp.where(hit, table[0, k], c)
            v = jnp.where(hit, table[1, k], v)
            g = jnp.where(hit, table[2, k], g)
        C[x] = c
        V[x] = v
        G[x] = 0.1 * g
        FE[0, x] = fraction(s0[x], v)
    for side in (0, 1):
        send_edge(side, FE.at[0, edge[side]], HF.at[0], sHF.at[0], rHF.at[0])

    lane = lax.broadcasted_iota(jnp.int32, (W, small.shape[1]), 1)

    def column(block, n):
        return jnp.sum(jnp.where(lane == n, block, 0.0), axis=1, keepdims=True)

    base = (i * (X * Z)).astype(jnp.float32)
    local_col = column(small[...], T + 1) - base
    cols = column(small[...], T + 2)
    pick_rows = jnp.where(
        lax.broadcasted_iota(jnp.int32, (W, X * Z), 1).astype(jnp.float32) == local_col, 1.0, 0.0
    )
    pick_cols = jnp.where(
        lax.broadcasted_iota(jnp.int32, (W, Y), 1).astype(jnp.float32) == cols, 1.0, 0.0
    )
    put_rows = jnp.where(
        lax.broadcasted_iota(jnp.int32, (X * Z, W), 0).astype(jnp.float32) == rows_row[...] - base,
        1.0, 0.0,
    )
    owned = jnp.sum(pick_rows, axis=1, keepdims=True)

    def tm_here(r, buf, ss, rs):
        @pl.when(r != t)
        def _():
            rdma(buf.at[r], buf.at[r], ss.at[1], rs.at[r], (r, i)).wait_recv()

    zi = lax.broadcasted_iota(jnp.int32, (Z, Y), 0)
    yi = lax.broadcasted_iota(jnp.int32, (Z, Y), 1)

    def coef(r):
        slot = lax.rem(r, 2)
        tm_here(r, SM, sS, rS)
        tm_here(r, M, sM, rM)
        for side in (0, 1):
            edge_here(side, MH.at[r], sMH.at[0], rMH.at[r])
        a = [PH[0] * MH[r, 0]] + [perm[t, x] * M[r, x] for x in range(X)] + [PH[1] * MH[r, 1]]
        for x in range(X + 1):
            TX[slot, x] = jnp.sqrt(a[x] * a[x + 1])
        for x in range(X):
            mid = a[x + 1]
            zp = jnp.where(zi < Z - 1, jnp.sqrt(mid * after(mid, 0)), 0.0)
            yp = jnp.where(yi < Y - 1, jnp.sqrt(mid * after(mid, 1)), 0.0)
            zm = before(zp, 0)
            ym = before(yp, 1)
            TZP[slot, x] = zp
            TZM[slot, x] = zm
            TYP[slot, x] = yp
            TYM[slot, x] = ym
            RC[slot, x] = 1.0 / (C[x] + (TX[slot, x] + TX[slot, x + 1] + zp + zm + yp + ym))
        rate = column(SM[r], 0)
        Q[slot] = jnp.dot(put_rows, pick_cols * rate, precision=EXACT).reshape(X, Z, Y)

    def start_step(r):
        slot = lax.rem(r, 2)
        tm_here(r, I, sI, rI)
        for x in range(X):
            B[x] = C[x] * PB[r * ITERS, x] + Q[slot, x] + I[r, x]

    def sweep(r, k):
        slot = lax.rem(r, 2)
        for n, x in enumerate(order):
            if x == 0:
                edge_here(0, HP.at[k], sHP.at[k], rHP.at[k])
                left = HP[k, 0]
            else:
                left = PB[k, x - 1]
            if x == X - 1:
                edge_here(1, HP.at[k], sHP.at[k], rHP.at[k])
                right = HP[k, 1]
            else:
                right = PB[k, x + 1]
            p = PB[k, x]
            total = B[x] + TX[slot, x] * left + TX[slot, x + 1] * right
            total = total + TZP[slot, x] * after(p, 0) + TZM[slot, x] * before(p, 0)
            total = total + TYP[slot, x] * after(p, 1) + TYM[slot, x] * before(p, 1)
            PB[k + 1, x] = total * RC[slot, x]
            if n < 2:
                send_edge(n, PB.at[k + 1, x], HP.at[k + 1], sHP.at[k + 1], rHP.at[k + 1])

    def put_out(r, src, out, which):
        @pl.when(r != t)
        def _():
            rdma(src, out.at[0, t], sO.at[r, which], rO.at[t, which], (r, i)).start()

        @pl.when(r == t)
        def _():
            pltpu.make_async_copy(src, out.at[0, t], lO.at[which]).start()

    def transport(r):
        slot = lax.rem(r, 2)
        k = (r + 1) * ITERS
        for side in (0, 1):
            edge_here(side, HF.at[r], sHF.at[r], rHF.at[r])

        def face(coupling, pi, pj, fi, fj):
            flux = coupling * (pi - pj)
            return flux * jnp.where(flux > 0, fi, fj)

        def p_of(x):
            return HP[k, 0] if x < 0 else (HP[k, 1] if x >= X else PB[k, x])

        def f_of(x):
            return HF[r, 0] if x < 0 else (HF[r, 1] if x >= X else FE[r, x])

        for x in order:
            p = p_of(x)
            f = f_of(x)
            s = SB[r, x]
            q = Q[slot, x]
            out = face(TX[slot, x + 1], p, p_of(x + 1), f, f_of(x + 1))
            out = out - face(TX[slot, x], p_of(x - 1), p, f_of(x - 1), f)
            cz = face(TZP[slot, x], p, after(p, 0), f, after(f, 0))
            cy = face(TYP[slot, x], p, after(p, 1), f, after(f, 1))
            out = out + (cz - before(cz, 0)) + (cy - before(cy, 1))
            gained = jnp.maximum(q, 0.0) * (1.0 - s) - jnp.maximum(-q, 0.0) * f - out
            s = s + G[x] * gained
            SB[r + 1, x] = s
            FE[r + 1, x] = fraction(s, V[x])
        put_out(r, SB.at[r + 1], outs, 1)

        @pl.when(r < R - 1)
        def _():
            for side in (0, 1):
                send_edge(side, FE.at[r + 1, edge[side]], HF.at[r + 1], sHF.at[r + 1], rHF.at[r + 1])

    for side in (0, 1):
        edge_here(side, PH, sPH, rPH)
    coef(0)
    ES[...] = jnp.zeros(ES.shape, jnp.float32)

    def step(r, carry):
        k = r * ITERS
        start_step(r)
        sweep(r, k)

        @pl.when(r > 0)
        def _():
            transport(r - 1)

        for j in range(1, ITERS):
            sweep(r, k + j)
            if j == 1:
                @pl.when(r < R - 1)
                def _():
                    coef(r + 1)
        put_out(r, PB.at[k + ITERS], outp, 0)
        seen = jnp.dot(pick_rows, PB[k + ITERS].reshape(X * Z, Y), precision=EXACT)
        predicted = jnp.sum(seen * pick_cols, axis=1, keepdims=True)
        gap = predicted - column(SM[r], 1 + t)
        ES[...] = ES[...] + owned * gap * gap
        return carry

    lax.fori_loop(0, R, step, 0)

    E0[...] = jnp.broadcast_to(jnp.sum(ES[...], axis=0, keepdims=True), E0.shape)
    others = [(d, lax.rem(i + d, N)) for d in range(1, N)]
    for d, peer in others:
        rdma(E0, E1.at[i], s1.at[d], r1.at[i], (t, peer)).start()
    for side in (0, 1):
        edge_here(side, HP.at[K], sHP.at[K], rHP.at[K])
    transport(R - 1)
    E1[i] = E0[...]
    for d, peer in others:
        rdma(E1.at[peer], E1.at[peer], s1.at[d], r1.at[peer], (t, peer)).wait_recv()
    whole = E1[0]
    for n in range(1, N):
        whole = whole + E1[n]
    mine = lax.broadcasted_iota(jnp.int32, whole.shape, 1) == t
    E2[t] = jnp.where(mine, whole, 0.0)
    for d, peer in peers():
        rdma(E2.at[t], E2.at[t], s2.at[d], r2.at[t], (peer, i)).start()
    for d, peer in peers():
        rdma(E2.at[peer], E2.at[peer], s2.at[d], r2.at[peer], (peer, i)).wait_recv()
    result = E2[0]
    for n in range(1, T):
        result = result + E2[n]
    mis[...] = result * (1.0 / (R * W))

    for side in (0, 1):
        edge_sent(side, p0.at[edge[side]], HP.at[0], sHP.at[0], rHP.at[0])
        edge_sent(side, perm.at[t, edge[side]], PH, sPH, rPH)
        edge_sent(side, mult.at[0, edge[side]], MH.at[t], sMH.at[0], rMH.at[t])

        def sent_k(k, c):
            edge_sent(side, PB.at[k, edge[side]], HP.at[k], sHP.at[k], rHP.at[k])
            return c

        lax.fori_loop(1, K + 1, sent_k, 0)

        def sent_r(r, c):
            edge_sent(side, FE.at[r, edge[side]], HF.at[r], sHF.at[r], rHF.at[r])
            return c

        lax.fori_loop(0, R, sent_r, 0)
    for d, peer in peers():
        rdma(small, SM.at[t], sS.at[d], rS.at[t], (peer, i)).wait_send()
        rdma(mult.at[0], M.at[t], sM.at[d], rM.at[t], (peer, i)).wait_send()
        rdma(infl.at[0], I.at[t], sI.at[d], rI.at[t], (peer, i)).wait_send()
        rdma(E2.at[t], E2.at[t], s2.at[d], r2.at[t], (peer, i)).wait_send()
        for side in (0, 1):
            edge_sent(side, mult.at[0, edge[side]], MH.at[t], sMH.at[d], rMH.at[t], peer)
    for d, peer in others:
        rdma(E0, E1.at[i], s1.at[d], r1.at[i], (t, peer)).wait_send()
    for d, peer in peers():
        for which, (src, out) in enumerate(((PB.at[K], outp), (SB.at[R], outs))):
            rdma(src, out.at[0, t], sO.at[peer, which], rO.at[t, which], (peer, i)).wait_send()
            rdma(src, out.at[0, peer], sO.at[peer, which], rO.at[peer, which], (peer, i)).wait_recv()
    for which, (src, out) in enumerate(((PB.at[K], outp), (SB.at[R], outs))):
        pltpu.make_async_copy(src, out.at[0, t], lO.at[which]).wait()


def body(
    perm_field, step_multiplier, inflow, start_pressure, start_saturation,
    region_ids, region_table, well_cells, well_rates, observed,
):
    T = lax.axis_size("tm")
    N = lax.axis_size("space")
    X, Z, Y = start_pressure.shape
    W = well_cells.shape[0]
    members = perm_field.shape[0]
    assert members == T and step_multiplier.shape[0] == 1
    well_row = (well_cells // Y).astype(jnp.float32)
    well_col = (well_cells % Y).astype(jnp.float32)
    small = jnp.concatenate(
        [well_rates, observed[:, 0, :], well_row[None], well_col[None]], axis=0
    ).T
    small = jnp.pad(small, ((0, 0), (0, 128 - small.shape[1])))
    K = T * ITERS
    f32 = jnp.float32
    cell = (Z, Y)
    block = (X, Z, Y)

    def buf(*shape):
        return pltpu.VMEM(shape, f32)

    dma = pltpu.SemaphoreType.DMA
    vmem = pl.BlockSpec(memory_space=pltpu.VMEM)
    anyspace = pl.BlockSpec(memory_space=pl.ANY)
    out_shape = jax.ShapeDtypeStruct((1, members) + block, f32)
    mis, outp, outs = pl.pallas_call(
        functools.partial(kernel, T, N),
        out_shape=(jax.ShapeDtypeStruct((8, 128), f32), out_shape, out_shape),
        in_specs=[vmem] * 6 + [pl.BlockSpec(memory_space=pltpu.SMEM)] + [vmem] * 2,
        out_specs=(vmem, anyspace, anyspace),
        scratch_shapes=[
            buf(T, *block), buf(T, *block), buf(T, W, 128), buf(T, 2, *cell), buf(2, *cell),
            buf(K + 1, 2, *cell), buf(T, 2, *cell), buf(K + 1, *block), buf(T + 1, *block),
            buf(T + 1, *block), buf(2, X + 1, *cell), buf(2, *block), buf(2, *block),
            buf(2, *block), buf(2, *block), buf(2, *block), buf(*block), buf(*block), buf(*block),
            buf(*block), buf(2, *block), buf(8, 128), buf(N, 8, 128), buf(T, 8, 128), buf(W, 1),
            dma((T,)), dma((T,)), dma((T,)), dma((T,)), dma((T,)), dma((T,)),
            dma((T, 2)), dma((T, 2)), dma((2,)), dma((2,)), dma((K + 1, 2)), dma((K + 1, 2)),
            dma((T, 2)), dma((T, 2)), dma((T, 2)), dma((T, 2)), dma((2,)),
            dma((N,)), dma((N,)), dma((T,)), dma((T,)),
        ],
        compiler_params=pltpu.CompilerParams(
            has_side_effects=True, vmem_limit_bytes=40 * 1024 * 1024
        ),
    )(
        perm_field, step_multiplier, inflow, start_pressure, start_saturation, region_ids,
        region_table, small, well_row[None],
    )
    return mis[0, :members], outp, outs


def solution(mesh):
    return jax.shard_map(
        body,
        mesh=mesh,
        in_specs=(
            P(None, "space", None, None),
            P("tm", "space", None, None),
            P("tm", "space", None, None),
            P("space", None, None),
            P("space", None, None),
            P("space", None, None),
            P(),
            P(),
            P("tm", None),
            P(None, "tm", None),
        ),
        out_specs=(P(), P("tm", None, "space", None, None), P("tm", None, "space", None, None)),
        check_vma=False,
    )
```

time: 283 us -> 82.2 us (0.29)
  starting transfers between devices: 119 us -> 0 us
  blocking collectives: 79.4 us -> 0 us
  Pallas kernels: 0 us -> 71.5 us
  other arithmetic: 33.1 us -> 0.02 us
  waiting for transfers between devices: 20.6 us -> 0 us
  matrix products: 17.5 us -> 0 us
  loops' own time: 3.42 us -> 0 us
    ppermute x32 -> x0, starting transfers between devices: 111 us -> none  [the longest x16 89.6 us: padded(): lax.ppermute(tail, axis, [(i, (i + 1) % count) for i in range(ends)])]
    pallas_call x0 -> x1, Pallas kernels: none -> 71.5 us  [body(): pl.pallas_call(functools.partial(kernel, T, N), out_shape=(jax.ShapeDtype...]
    psum x1 -> x0, blocking collectives: 46.4 us -> none  [body(): totals = lax.psum(misfit, ('tm', 'space'))]
    all_gather x3 -> x0, blocking collectives: 20.7 us -> none  [the longest x1 8.19 us: body(): lax.all_gather(inflow, 'tm', axis=0, tiled=True)]
    ppermute x32 -> x0, waiting for transfers between devices: 20.6 us -> none  [the longest x16 18.9 us: padded(): lax.ppermute(tail, axis, [(i, (i + 1) % count) for i in range(ends)])]
    dot_general x5 -> x0, matrix products: 17.5 us -> none  [the longest x4 16.2 us: mismatch(): jnp.dot(pressure.reshape(batch_size, -1), well_picks.T, precision=lax.Pre...]
    all_to_all x1 -> x0, blocking collectives: 12.3 us -> none  [body(): lax.all_to_all(result[2], 'tm', split_axis=0, concat_axis=1, tiled=True)]
    add x3 -> x0, other arithmetic: 10.4 us -> none  [the longest x2 10.3 us: region_fields(): summed + jnp.where(region_ids == region_index, region_table[table_row, re...]
  transfers between devices with their start and end apart: 34 -> 0, of which waited for: 17 -> 0; matrix products, arithmetic and copies ran while one was open for 13% -> 0% of each run, Pallas kernels for 0% -> 0%
where the time goes in v1:
time: 82.2 us; the launch traced here: 81.9 us
  Pallas kernels  71.5 us (87%)
  local copies, waits for them, and re-layouts  9.75 us (12%)
    pallas_call x1, Pallas kernels, body(): pl.pallas_call(functools.partial(kernel, T, N), out_shape=(jax.ShapeDtype...  71.5 us
    unnamed x22, local copies, waits for them, and re-layouts  9.14 us

profile of v1, /device:TPU:0, one launch (start us, length us, event | category | flops | bytes accessed | tf_op | source)
XLA Modules:
  0.0 81.9 jit_solution(8088178446518905712)
XLA Ops:
  0.6 0.0 copy-start.9
  0.6 0.6 copy-done.9
  1.3 0.0 copy-start.7
  1.3 0.0 copy-start.8
  1.3 0.7 copy-done.7
  2.0 0.0 copy-done.8
  2.0 0.1 copy.17
  2.1 0.0 copy-start.6
  2.1 0.7 copy-done.6
  2.8 0.0 copy-start
  2.8 1.0 %copy-done = f32[4,4,32,256]{3,2,1,0:T(8,128)S(1)} copy-done((f32[4,4,32,256]{3,2,1,0:T(8,128)S(1)}, f32[4,4,32,256]{3,2,1,0:T(8,128)}, u32[]{:S(2)}) %copy-start) | copy-done | bytes 524312
  3.8 0.0 copy-start.1
  3.8 0.9 %copy-done.1 = f32[1,4,32,256]{3,2,1,0:T(8,128)S(1)} copy-done((f32[1,4,32,256]{3,2,1,0:T(8,128)S(1)}, f32[1,4,32,256]{3,2,1,0:T(8,128)}, u32[]{:S(2)}) %copy-start.1) | copy-done | bytes 131096
  4.7 0.0 copy-start.2
  4.7 0.9 %copy-done.2 = f32[1,4,32,256]{3,2,1,0:T(8,128)S(1)} copy-done((f32[1,4,32,256]{3,2,1,0:T(8,128)S(1)}, f32[1,4,32,256]{3,2,1,0:T(8,128)}, u32[]{:S(2)}) %copy-start.2) | copy-done | bytes 131096
  5.6 0.0 copy-start.3
  5.6 0.9 %copy-done.3 = f32[4,32,256]{2,1,0:T(8,128)S(1)} copy-done((f32[4,32,256]{2,1,0:T(8,128)S(1)}, f32[4,32,256]{2,1,0:T(8,128)}, u32[]{:S(2)}) %copy-start.3) | copy-done | bytes 131096
  6.5 0.0 copy-start.4
  6.5 0.9 %copy-done.4 = f32[4,32,256]{2,1,0:T(8,128)S(1)} copy-done((f32[4,32,256]{2,1,0:T(8,128)S(1)}, f32[4,32,256]{2,1,0:T(8,128)}, u32[]{:S(2)}) %copy-start.4) | copy-done | bytes 131096
  7.4 0.0 copy-start.5
  7.4 0.9 %copy-done.5 = s32[4,32,256]{2,1,0:T(8,128)S(1)} copy-done((s32[4,32,256]{2,1,0:T(8,128)S(1)}, s32[4,32,256]{2,1,0:T(8,128)}, u32[]{:S(2)}) %copy-start.5) | copy-done | bytes 131096
  8.3 71.5 %shard_map.121 = (f32[8,128]{1,0:T(8,128)S(1)}, f32[1,4,4,32,256]{4,3,2,1,0:T(8,128)S(1)}, f32[1,4,4,32,256]{4,3,2,1,0:T(8,128)S(1)}) custom-call(f32[4,4,32,256]{3,2,1,0:T(8,128)S(1)} %copy-done, f32[1,4,32,256]{3,2,1,0:T(8,128)S(1)} %copy-done.1, f32[1,4,32,256]{3,2,1,0:T(8,128)S(1)} %copy-done.2, f32[4,32,256]{2,1,0:T(8,128)S(1)} %copy-done.3, ...), custom_call_target="tpu_custom_call" | custom-call | tf_op jit(solution)/shard_map/pallas_call | solution.py:367
  79.8 0.5 slice_bitcast_fusion
  80.3 0.8 copy.20
  81.1 0.8 copy.21
  (3 shorter events, 0.0 us)
Async XLA Ops:
  0.6 0.7 copy-start.9
  1.3 0.7 copy-start.7
  1.3 0.7 copy-start.8
  2.1 0.7 copy-start.6
  2.8 1.0 %copy-start = (f32[4,4,32,256]{3,2,1,0:T(8,128)S(1)}, f32[4,4,32,256]{3,2,1,0:T(8,128)}, u32[]{:S(2)}) copy-start(f32[4,4,32,256]{3,2,1,0:T(8,128)} %perm.1) | copy-start | bytes 1572868
  3.8 0.9 %copy-start.1 = (f32[1,4,32,256]{3,2,1,0:T(8,128)S(1)}, f32[1,4,32,256]{3,2,1,0:T(8,128)}, u32[]{:S(2)}) copy-start(f32[1,4,32,256]{3,2,1,0:T(8,128)} %mult.1) | copy-start | bytes 393220
  4.7 0.9 %copy-start.2 = (f32[1,4,32,256]{3,2,1,0:T(8,128)S(1)}, f32[1,4,32,256]{3,2,1,0:T(8,128)}, u32[]{:S(2)}) copy-start(f32[1,4,32,256]{3,2,1,0:T(8,128)} %infl.1) | copy-start | bytes 393220
  5.6 0.9 %copy-start.3 = (f32[4,32,256]{2,1,0:T(8,128)S(1)}, f32[4,32,256]{2,1,0:T(8,128)}, u32[]{:S(2)}) copy-start(f32[4,32,256]{2,1,0:T(8,128)} %p0.1) | copy-start | bytes 393220
  6.5 0.9 %copy-start.4 = (f32[4,32,256]{2,1,0:T(8,128)S(1)}, f32[4,32,256]{2,1,0:T(8,128)}, u32[]{:S(2)}) copy-start(f32[4,32,256]{2,1,0:T(8,128)} %s0.1) | copy-start | bytes 393220
  7.4 0.9 %copy-start.5 = (s32[4,32,256]{2,1,0:T(8,128)S(1)}, s32[4,32,256]{2,1,0:T(8,128)}, u32[]{:S(2)}) copy-start(s32[4,32,256]{2,1,0:T(8,128)} %ids.1) | copy-start | bytes 393220

commit v2 on v1

--- a/solution.py
+++ b/solution.py
@@ -24,13 +24,23 @@
     T, N,
     perm, mult, infl, p0, s0, ids, table, small, rows_row,
     mis, outp, outs,
-    M, I, SM, MH, PH, HP, HF, PB, SB, FE, TX, TZP, TZM, TYP, TYM, RC, C, V, G, B, Q, E0, E1, E2, ES,
+    PM, IDS, M, I, SM, MH, PH, HP, HF, PB, SB, FE, TX, TZP, TZM, TYP, TYM, RC, C, V, G, B, Q, E0, E1, E2, ES,
     sM, rM, sI, rI, sS, rS, sMH, rMH, sPH, rPH, sHP, rHP, sHF, rHF, sO, rO, lO, s1, r1, s2, r2,
+    fM, fI, fMH, lIN,
 ):
     t = lax.axis_index("tm")
     i = lax.axis_index("space")
-    X, Z, Y = p0.shape
+    X, Z, Y = IDS.shape
     R = T
+    loads = [
+        pltpu.make_async_copy(src, dst, lIN.at[n])
+        for n, (src, dst) in enumerate((
+            (mult.at[0], M.at[t]), (p0, PB.at[0]), (perm.at[t], PM), (infl.at[0], I.at[t]),
+            (ids, IDS), (s0, SB.at[0]),
+        ))
+    ]
+    for load in loads:
+        load.start()
     W = small.shape[0]
     K = R * ITERS
     has = (i > 0, i < N - 1)
@@ -67,17 +77,72 @@
     def peers():
         return [(d, lax.rem(t + d, T)) for d in range(1, T)]
 
-    for side in (0, 1):
-        send_edge(side, p0.at[edge[side]], HP.at[0], sHP.at[0], rHP.at[0])
-        send_edge(side, perm.at[t, edge[side]], PH, sPH, rPH)
-        send_edge(side, mult.at[0, edge[side]], MH.at[t], sMH.at[0], rMH.at[t])
+    barrier = pltpu.get_barrier_semaphore()
+
+    def greet(device):
+        pl.semaphore_signal(barrier, inc=1, device_id=device, device_id_type=MESH)
+
+    for d, peer in peers():
+        greet((peer, i))
+    for d in range(1, N):
+        greet((t, lax.rem(i + d, N)))
+    for side in (0, 1):
+        @pl.when(has[side])
+        def _():
+            for d, peer in peers():
+                greet((peer, beside[side]))
+
+    sides = jnp.where(has[0], 1, 0) + jnp.where(has[1], 1, 0)
+    pl.semaphore_wait(barrier, (N - 1) + (T - 1) + (T - 1) * sides)
+
+    mate = t + 1 - 2 * lax.rem(t, 2)
+
+    def targets():
+        return [(0, mate)] + [(d, lax.rem(t + 2 * d, T)) for d in range(1, T // 2)]
+
+    def send_fields():
+        for d, peer in targets():
+            rdma(M.at[t], M.at[t], sM.at[d], rM.at[t], (peer, i)).start()
+        for side in (0, 1):
+            for d, peer in targets():
+                send_edge(side, M.at[t, edge[side]], MH.at[t], sMH.at[d + 1], rMH.at[t], peer)
+        for d, peer in targets():
+            rdma(I.at[t], I.at[t], sI.at[d], rI.at[t], (peer, i)).start()
+
+    def passes_on(r):
+        return jnp.logical_and(lax.rem(t, 2) == lax.rem(r, 2), t != r)
+
+    def pass_on(r):
+        @pl.when(passes_on(r))
+        def _():
+            rdma(M.at[r], M.at[r], sM.at[1], rM.at[r], (r, i)).wait_recv()
+            rdma(M.at[r], M.at[r], fM.at[r], rM.at[r], (mate, i)).start()
+            for side in (0, 1):
+                edge_here(side, MH.at[r], sMH.at[0], rMH.at[r])
+
+                @pl.when(has[side])
+                def _():
+                    rdma(
+                        MH.at[r, side], MH.at[r, side], fMH.at[r, side], rMH.at[r, side], (mate, i)
+                    ).start()
+            rdma(I.at[r], I.at[r], sI.at[1], rI.at[r], (r, i)).wait_recv()
+            rdma(I.at[r], I.at[r], fI.at[r], rI.at[r], (mate, i)).start()
+
+    for n in range(3):
+        loads[n].wait()
+    for side in (0, 1):
+        send_edge(side, M.at[t, edge[side]], MH.at[t], sMH.at[0], rMH.at[t])
+    loads[3].wait()
+
+    @pl.when(t == 0)
+    def _():
+        send_fields()
+
+    for side in (0, 1):
+        send_edge(side, PM.at[edge[side]], PH, sPH, rPH)
+        send_edge(side, PB.at[0, edge[side]], HP.at[0], sHP.at[0], rHP.at[0])
     for d, peer in peers():
         rdma(small, SM.at[t], sS.at[d], rS.at[t], (peer, i)).start()
-        rdma(mult.at[0], M.at[t], sM.at[d], rM.at[t], (peer, i)).start()
-        for side in (0, 1):
-            send_edge(side, mult.at[0, edge[side]], MH.at[t], sMH.at[d], rMH.at[t], peer)
-    for d, peer in peers():
-        rdma(infl.at[0], I.at[t], sI.at[d], rI.at[t], (peer, i)).start()
 
     for side in (0, 1):
         @pl.when(jnp.logical_not(has[side]))
@@ -98,11 +163,9 @@
 
             lax.fori_loop(0, R, clear_r, 0)
 
-    M[t] = mult[0]
-    I[t] = infl[0]
     SM[t] = small[...]
-    PB[0] = p0[...]
-    SB[0] = s0[...]
+    loads[4].wait()
+    loads[5].wait()
 
     def fraction(s, v):
         sq = s * s
@@ -110,7 +173,7 @@
         return sq / (sq + v * rest)
 
     for x in order:
-        rock = ids[x]
+        rock = IDS[x]
         c = jnp.zeros((Z, Y), jnp.float32)
         v = c
         g = c
@@ -122,7 +185,7 @@
         C[x] = c
         V[x] = v
         G[x] = 0.1 * g
-        FE[0, x] = fraction(s0[x], v)
+        FE[0, x] = fraction(SB[0, x], v)
     for side in (0, 1):
         send_edge(side, FE.at[0, edge[side]], HF.at[0], sHF.at[0], rHF.at[0])
 
@@ -157,10 +220,14 @@
     def coef(r):
         slot = lax.rem(r, 2)
         tm_here(r, SM, sS, rS)
-        tm_here(r, M, sM, rM)
-        for side in (0, 1):
-            edge_here(side, MH.at[r], sMH.at[0], rMH.at[r])
-        a = [PH[0] * MH[r, 0]] + [perm[t, x] * M[r, x] for x in range(X)] + [PH[1] * MH[r, 1]]
+
+        @pl.when(jnp.logical_not(passes_on(r)))
+        def _():
+            tm_here(r, M, sM, rM)
+            for side in (0, 1):
+                edge_here(side, MH.at[r], sMH.at[0], rMH.at[r])
+
+        a = [PH[0] * MH[r, 0]] + [PM[x] * M[r, x] for x in range(X)] + [PH[1] * MH[r, 1]]
         for x in range(X + 1):
             TX[slot, x] = jnp.sqrt(a[x] * a[x + 1])
         for x in range(X):
@@ -179,7 +246,11 @@
 
     def start_step(r):
         slot = lax.rem(r, 2)
-        tm_here(r, I, sI, rI)
+
+        @pl.when(jnp.logical_not(passes_on(r)))
+        def _():
+            tm_here(r, I, sI, rI)
+
         for x in range(X):
             B[x] = C[x] * PB[r * ITERS, x] + Q[slot, x] + I[r, x]
 
@@ -204,21 +275,29 @@
             if n < 2:
                 send_edge(n, PB.at[k + 1, x], HP.at[k + 1], sHP.at[k + 1], rHP.at[k + 1])
 
-    def put_out(r, src, out, which):
+    parts = ((0, 0, X), (1, 1, X - 2), (2, 0, 1), (3, X - 1, 1))
+
+    def piece(which, r, member):
+        _, at, many = parts[which]
+        rows = pl.ds(at, many)
+        if which == 0:
+            return PB.at[(r + 1) * ITERS, rows], outp.at[0, member, rows]
+        return SB.at[r + 1, rows], outs.at[0, member, rows]
+
+    def put_out(r, which):
+        src, dst = piece(which, r, t)
+
         @pl.when(r != t)
         def _():
-            rdma(src, out.at[0, t], sO.at[r, which], rO.at[t, which], (r, i)).start()
+            rdma(src, dst, sO.at[r, which], rO.at[t, which], (r, i)).start()
 
         @pl.when(r == t)
         def _():
-            pltpu.make_async_copy(src, out.at[0, t], lO.at[which]).start()
-
-    def transport(r):
+            pltpu.make_async_copy(src, dst, lO.at[which]).start()
+
+    def transport(r, last=False):
         slot = lax.rem(r, 2)
         k = (r + 1) * ITERS
-        for side in (0, 1):
-            edge_here(side, HF.at[r], sHF.at[r], rHF.at[r])
-
         def face(coupling, pi, pj, fi, fj):
             flux = coupling * (pi - pj)
             return flux * jnp.where(flux > 0, fi, fj)
@@ -229,7 +308,14 @@
         def f_of(x):
             return HF[r, 0] if x < 0 else (HF[r, 1] if x >= X else FE[r, x])
 
-        for x in order:
+        for x in order[2:] + order[:2]:
+            if x in edge:
+                side = edge.index(x)
+                if side == 0:
+                    put_out(r, 1)
+                edge_here(side, HF.at[r], sHF.at[r], rHF.at[r])
+                if last:
+                    edge_here(side, HP.at[k], sHP.at[k], rHP.at[k])
             p = p_of(x)
             f = f_of(x)
             s = SB[r, x]
@@ -242,13 +328,21 @@
             gained = jnp.maximum(q, 0.0) * (1.0 - s) - jnp.maximum(-q, 0.0) * f - out
             s = s + G[x] * gained
             SB[r + 1, x] = s
-            FE[r + 1, x] = fraction(s, V[x])
-        put_out(r, SB.at[r + 1], outs, 1)
+            if not last:
+                FE[r + 1, x] = fraction(s, V[x])
+            if x in edge:
+                put_out(r, 2 + edge.index(x))
 
         @pl.when(r < R - 1)
         def _():
             for side in (0, 1):
                 send_edge(side, FE.at[r + 1, edge[side]], HF.at[r + 1], sHF.at[r + 1], rHF.at[r + 1])
+
+    pass_on(0)
+
+    @pl.when(t > 0)
+    def _():
+        send_fields()
 
     for side in (0, 1):
         edge_here(side, PH, sPH, rPH)
@@ -263,6 +357,10 @@
         @pl.when(r > 0)
         def _():
             transport(r - 1)
+
+        @pl.when(r < R - 1)
+        def _():
+            pass_on(r + 1)
 
         for j in range(1, ITERS):
             sweep(r, k + j)
@@ -270,7 +368,7 @@
                 @pl.when(r < R - 1)
                 def _():
                     coef(r + 1)
-        put_out(r, PB.at[k + ITERS], outp, 0)
+        put_out(r, 0)
         seen = jnp.dot(pick_rows, PB[k + ITERS].reshape(X * Z, Y), precision=EXACT)
         predicted = jnp.sum(seen * pick_cols, axis=1, keepdims=True)
         gap = predicted - column(SM[r], 1 + t)
@@ -283,9 +381,7 @@
     others = [(d, lax.rem(i + d, N)) for d in range(1, N)]
     for d, peer in others:
         rdma(E0, E1.at[i], s1.at[d], r1.at[i], (t, peer)).start()
-    for side in (0, 1):
-        edge_here(side, HP.at[K], sHP.at[K], rHP.at[K])
-    transport(R - 1)
+    transport(R - 1, True)
     E1[i] = E0[...]
     for d, peer in others:
         rdma(E1.at[peer], E1.at[peer], s1.at[d], r1.at[peer], (t, peer)).wait_recv()
@@ -304,36 +400,53 @@
     mis[...] = result * (1.0 / (R * W))
 
     for side in (0, 1):
-        edge_sent(side, p0.at[edge[side]], HP.at[0], sHP.at[0], rHP.at[0])
-        edge_sent(side, perm.at[t, edge[side]], PH, sPH, rPH)
-        edge_sent(side, mult.at[0, edge[side]], MH.at[t], sMH.at[0], rMH.at[t])
+        edge_sent(side, M.at[t, edge[side]], MH.at[t], sMH.at[0], rMH.at[t])
+        edge_sent(side, PM.at[edge[side]], PH, sPH, rPH)
 
         def sent_k(k, c):
             edge_sent(side, PB.at[k, edge[side]], HP.at[k], sHP.at[k], rHP.at[k])
             return c
 
-        lax.fori_loop(1, K + 1, sent_k, 0)
+        lax.fori_loop(0, K + 1, sent_k, 0)
 
         def sent_r(r, c):
             edge_sent(side, FE.at[r, edge[side]], HF.at[r], sHF.at[r], rHF.at[r])
+
+            @pl.when(jnp.logical_and(passes_on(r), has[side]))
+            def _():
+                rdma(
+                    MH.at[r, side], MH.at[r, side], fMH.at[r, side], rMH.at[r, side], (mate, i)
+                ).wait_send()
             return c
 
         lax.fori_loop(0, R, sent_r, 0)
+        for d, peer in targets():
+            edge_sent(side, M.at[t, edge[side]], MH.at[t], sMH.at[d + 1], rMH.at[t], peer)
+
+    def sent_on(r, c):
+        @pl.when(passes_on(r))
+        def _():
+            rdma(M.at[r], M.at[r], fM.at[r], rM.at[r], (mate, i)).wait_send()
+            rdma(I.at[r], I.at[r], fI.at[r], rI.at[r], (mate, i)).wait_send()
+        return c
+
+    lax.fori_loop(0, R, sent_on, 0)
+    for d, peer in targets():
+        rdma(M.at[t], M.at[t], sM.at[d], rM.at[t], (peer, i)).wait_send()
+        rdma(I.at[t], I.at[t], sI.at[d], rI.at[t], (peer, i)).wait_send()
     for d, peer in peers():
         rdma(small, SM.at[t], sS.at[d], rS.at[t], (peer, i)).wait_send()
-        rdma(mult.at[0], M.at[t], sM.at[d], rM.at[t], (peer, i)).wait_send()
-        rdma(infl.at[0], I.at[t], sI.at[d], rI.at[t], (peer, i)).wait_send()
         rdma(E2.at[t], E2.at[t], s2.at[d], r2.at[t], (peer, i)).wait_send()
-        for side in (0, 1):
-            edge_sent(side, mult.at[0, edge[side]], MH.at[t], sMH.at[d], rMH.at[t], peer)
     for d, peer in others:
         rdma(E0, E1.at[i], s1.at[d], r1.at[i], (t, peer)).wait_send()
-    for d, peer in peers():
-        for which, (src, out) in enumerate(((PB.at[K], outp), (SB.at[R], outs))):
-            rdma(src, out.at[0, t], sO.at[peer, which], rO.at[t, which], (peer, i)).wait_send()
-            rdma(src, out.at[0, peer], sO.at[peer, which], rO.at[peer, which], (peer, i)).wait_recv()
-    for which, (src, out) in enumerate(((PB.at[K], outp), (SB.at[R], outs))):
-        pltpu.make_async_copy(src, out.at[0, t], lO.at[which]).wait()
+    for which in range(len(parts)):
+        for d, peer in peers():
+            src, dst = piece(which, peer, t)
+            rdma(src, dst, sO.at[peer, which], rO.at[t, which], (peer, i)).wait_send()
+            src, dst = piece(which, t, peer)
+            rdma(src, dst, sO.at[peer, which], rO.at[peer, which], (peer, i)).wait_recv()
+        src, dst = piece(which, t, t)
+        pltpu.make_async_copy(src, dst, lO.at[which]).wait()
 
 
 def body(
@@ -345,7 +458,7 @@
     X, Z, Y = start_pressure.shape
     W = well_cells.shape[0]
     members = perm_field.shape[0]
-    assert members == T and step_multiplier.shape[0] == 1
+    assert members == T and T % 2 == 0 and step_multiplier.shape[0] == 1
     well_row = (well_cells // Y).astype(jnp.float32)
     well_col = (well_cells % Y).astype(jnp.float32)
     small = jnp.concatenate(
@@ -367,9 +480,10 @@
     mis, outp, outs = pl.pallas_call(
         functools.partial(kernel, T, N),
         out_shape=(jax.ShapeDtypeStruct((8, 128), f32), out_shape, out_shape),
-        in_specs=[vmem] * 6 + [pl.BlockSpec(memory_space=pltpu.SMEM)] + [vmem] * 2,
+        in_specs=[anyspace] * 6 + [pl.BlockSpec(memory_space=pltpu.SMEM)] + [vmem] * 2,
         out_specs=(vmem, anyspace, anyspace),
         scratch_shapes=[
+            buf(*block), pltpu.VMEM(block, jnp.int32),
             buf(T, *block), buf(T, *block), buf(T, W, 128), buf(T, 2, *cell), buf(2, *cell),
             buf(K + 1, 2, *cell), buf(T, 2, *cell), buf(K + 1, *block), buf(T + 1, *block),
             buf(T + 1, *block), buf(2, X + 1, *cell), buf(2, *block), buf(2, *block),
@@ -377,11 +491,12 @@
             buf(*block), buf(2, *block), buf(8, 128), buf(N, 8, 128), buf(T, 8, 128), buf(W, 1),
             dma((T,)), dma((T,)), dma((T,)), dma((T,)), dma((T,)), dma((T,)),
             dma((T, 2)), dma((T, 2)), dma((2,)), dma((2,)), dma((K + 1, 2)), dma((K + 1, 2)),
-            dma((T, 2)), dma((T, 2)), dma((T, 2)), dma((T, 2)), dma((2,)),
+            dma((T, 2)), dma((T, 2)), dma((T, 4)), dma((T, 4)), dma((4,)),
             dma((N,)), dma((N,)), dma((T,)), dma((T,)),
+            dma((T,)), dma((T,)), dma((T, 2)), dma((6,)),
         ],
         compiler_params=pltpu.CompilerParams(
-            has_side_effects=True, vmem_limit_bytes=40 * 1024 * 1024
+            has_side_effects=True, collective_id=0
         ),
     )(
         perm_field, step_multiplier, inflow, start_pressure, start_saturation, region_ids,

time: 82.2 us -> 72.9 us (0.89)
  Pallas kernels: 71.5 us -> 66 us
  local copies, waits for them, and re-layouts: 9.75 us -> 5.95 us
    pallas_call x1, Pallas kernels: 71.5 us -> 66 us  [body(): pl.pallas_call(functools.partial(kernel, T, N), out_shape=(jax.ShapeDtype...]
    unnamed x22 -> x12, local copies, waits for them, and re-layouts: 9.14 us -> 4.06 us
where the time goes in v2:
time: 72.9 us; the launch traced here: 72.7 us
  Pallas kernels  66 us (91%)
  local copies, waits for them, and re-layouts  5.95 us (8%)
    pallas_call x1, Pallas kernels, body(): pl.pallas_call(functools.partial(kernel, T, N), out_shape=(jax.ShapeDtype...  66 us
    unnamed x12, local copies, waits for them, and re-layouts  4.06 us

profile of v2, /device:TPU:0, one launch (start us, length us, event | category | flops | bytes accessed | tf_op | source)
XLA Modules:
  0.0 72.7 jit_solution(4763355131174911716)
XLA Ops:
  0.6 0.0 copy-start.4
  0.6 0.6 copy-done.4
  1.3 0.0 copy-start.1
  1.3 0.0 copy-start.2
  1.3 0.0 copy-start.3
  1.3 0.5 copy-done.1
  1.8 0.2 copy-done.2
  2.0 0.0 copy-done.3
  2.0 0.1 copy.17
  2.1 0.6 pad.4.small
  2.7 66.0 %shard_map.121 = (f32[8,128]{1,0:T(8,128)}, f32[1,4,4,32,256]{4,3,2,1,0:T(8,128)}, f32[1,4,4,32,256]{4,3,2,1,0:T(8,128)}) custom-call(f32[4,4,32,256]{3,2,1,0:T(8,128)} %perm.1, f32[1,4,32,256]{3,2,1,0:T(8,128)} %mult.1, f32[1,4,32,256]{3,2,1,0:T(8,128)} %infl.1, f32[4,32,256]{2,1,0:T(8,128)} %p0.1, f32[4,32,256]{2,1,0:T(8,128)} %s0.1, s32[4,32,256]{2,1,0:T(8,128)} %ids.1, ...), custom_call_target="tpu_custom_call" | custom-call | tf_op jit(solution)/shard_map/pallas_call | solution.py:480
  68.8 1.2 %slice_bitcast_fusion = f32[4]{0:T(128)} fusion(f32[8,128]{1,0:T(8,128)} %get-tuple-element.6), kind=kLoop, calls=%fused_computation.8 | loop fusion | bytes 32 | tf_op jit(solution)/shard_map/squeeze | solution.py:505
  70.0 0.0 copy-start
  70.0 1.9 %copy.20 = f32[1,4,4,32,256]{4,3,2,1,0:T(8,128)} copy(f32[1,4,4,32,256]{4,3,2,1,0:T(8,128)} %get-tuple-element.15) | data formatting | bytes 1048576
  71.9 0.0 copy-done
  71.9 0.8 %copy.21 = f32[1,4,4,32,256]{4,3,2,1,0:T(8,128)} copy(f32[1,4,4,32,256]{4,3,2,1,0:T(8,128)S(1)} %copy-done) | data formatting | bytes 1048576
  (2 shorter events, 0.0 us)
Async XLA Ops:
  0.6 0.7 copy-start.4
  1.3 0.5 copy-start.1
  1.3 0.7 copy-start.2
  1.3 0.7 copy-start.3
  70.0 1.9 %copy-start = (f32[1,4,4,32,256]{4,3,2,1,0:T(8,128)S(1)}, f32[1,4,4,32,256]{4,3,2,1,0:T(8,128)}, u32[]{:S(2)}) copy-start(f32[1,4,4,32,256]{4,3,2,1,0:T(8,128)} %get-tuple-element.16) | copy-start | bytes 1572868

commit v3 on v2

--- a/solution.py
+++ b/solution.py
@@ -24,9 +24,9 @@
     T, N,
     perm, mult, infl, p0, s0, ids, table, small, rows_row,
     mis, outp, outs,
-    PM, IDS, M, I, SM, MH, PH, HP, HF, PB, SB, FE, TX, TZP, TZM, TYP, TYM, RC, C, V, G, B, Q, E0, E1, E2, ES,
+    PM, IDS, IH, M, I, SM, MH, PH, HP, HF, PB, SB, FE, TX, TZP, TZM, TYP, TYM, RC, C, V, G, B, Q, E0, E1, E2, ES,
     sM, rM, sI, rI, sS, rS, sMH, rMH, sPH, rPH, sHP, rHP, sHF, rHF, sO, rO, lO, s1, r1, s2, r2,
-    fM, fI, fMH, lIN,
+    fM, fI, fMH, lIN, sIH, rIH, fIH, sC, rC,
 ):
     t = lax.axis_index("tm")
     i = lax.axis_index("space")
@@ -46,6 +46,7 @@
     has = (i > 0, i < N - 1)
     beside = (i - 1, i + 1)
     edge = (0, X - 1)
+    two = (pl.ds(0, 2), pl.ds(X - 2, 2))
     order = [0, X - 1] + list(range(1, X - 1))
 
     def rdma(src, dst, ss, rs, dev):
@@ -105,7 +106,8 @@
             rdma(M.at[t], M.at[t], sM.at[d], rM.at[t], (peer, i)).start()
         for side in (0, 1):
             for d, peer in targets():
-                send_edge(side, M.at[t, edge[side]], MH.at[t], sMH.at[d + 1], rMH.at[t], peer)
+                send_edge(side, M.at[t, two[side]], MH.at[t], sMH.at[d + 1], rMH.at[t], peer)
+                send_edge(side, I.at[t, edge[side]], IH.at[t], sIH.at[d + 1], rIH.at[t], peer)
         for d, peer in targets():
             rdma(I.at[t], I.at[t], sI.at[d], rI.at[t], (peer, i)).start()
 
@@ -125,22 +127,30 @@
                     rdma(
                         MH.at[r, side], MH.at[r, side], fMH.at[r, side], rMH.at[r, side], (mate, i)
                     ).start()
+                edge_here(side, IH.at[r], sIH.at[0], rIH.at[r])
+
+                @pl.when(has[side])
+                def _():
+                    rdma(
+                        IH.at[r, side], IH.at[r, side], fIH.at[r, side], rIH.at[r, side], (mate, i)
+                    ).start()
             rdma(I.at[r], I.at[r], sI.at[1], rI.at[r], (r, i)).wait_recv()
             rdma(I.at[r], I.at[r], fI.at[r], rI.at[r], (mate, i)).start()
 
     for n in range(3):
         loads[n].wait()
-    for side in (0, 1):
-        send_edge(side, M.at[t, edge[side]], MH.at[t], sMH.at[0], rMH.at[t])
     loads[3].wait()
+    for side in (0, 1):
+        send_edge(side, M.at[t, two[side]], MH.at[t], sMH.at[0], rMH.at[t])
+        send_edge(side, I.at[t, edge[side]], IH.at[t], sIH.at[0], rIH.at[t])
 
     @pl.when(t == 0)
     def _():
         send_fields()
 
     for side in (0, 1):
-        send_edge(side, PM.at[edge[side]], PH, sPH, rPH)
-        send_edge(side, PB.at[0, edge[side]], HP.at[0], sHP.at[0], rHP.at[0])
+        send_edge(side, PM.at[two[side]], PH, sPH, rPH)
+        send_edge(side, PB.at[0, two[side]], HP.at[0], sHP.at[0], rHP.at[0])
     for d, peer in peers():
         rdma(small, SM.at[t], sS.at[d], rS.at[t], (peer, i)).start()
 
@@ -148,17 +158,19 @@
         @pl.when(jnp.logical_not(has[side]))
         def _():
             zero = jnp.zeros((Z, Y), jnp.float32)
-            PH[side] = zero
+            PH[side] = jnp.zeros((2, Z, Y), jnp.float32)
+            C[(0, X + 1)[side]] = zero + 1.0
 
             def clear(n, c):
-                HP[n, side] = zero
+                HP[n, side] = jnp.zeros((2, Z, Y), jnp.float32)
                 return c
 
             lax.fori_loop(0, K + 1, clear, 0)
 
             def clear_r(n, c):
                 HF[n, side] = zero
-                MH[n, side] = zero
+                MH[n, side] = jnp.zeros((2, Z, Y), jnp.float32)
+                IH[n, side] = zero
                 return c
 
             lax.fori_loop(0, R, clear_r, 0)
@@ -182,12 +194,23 @@
             c = jnp.where(hit, table[0, k], c)
             v = jnp.where(hit, table[1, k], v)
             g = jnp.where(hit, table[2, k], g)
-        C[x] = c
+        C[x + 1] = c
         V[x] = v
         G[x] = 0.1 * g
         FE[0, x] = fraction(SB[0, x], v)
     for side in (0, 1):
         send_edge(side, FE.at[0, edge[side]], HF.at[0], sHF.at[0], rHF.at[0])
+
+    def storage_edge(side):
+        return rdma(
+            C.at[edge[side] + 1], C.at[(X + 1, 0)[side]], sC.at[side], rC.at[1 - side],
+            (t, beside[side]),
+        )
+
+    for side in (0, 1):
+        @pl.when(has[side])
+        def _():
+            storage_edge(side).start()
 
     lane = lax.broadcasted_iota(jnp.int32, (W, small.shape[1]), 1)
 
@@ -204,7 +227,8 @@
         lax.broadcasted_iota(jnp.int32, (W, Y), 1).astype(jnp.float32) == cols, 1.0, 0.0
     )
     put_rows = jnp.where(
-        lax.broadcasted_iota(jnp.int32, (X * Z, W), 0).astype(jnp.float32) == rows_row[...] - base,
+        lax.broadcasted_iota(jnp.int32, ((X + 2) * Z, W), 0).astype(jnp.float32)
+        == rows_row[...] - base + float(Z),
         1.0, 0.0,
     )
     owned = jnp.sum(pick_rows, axis=1, keepdims=True)
@@ -226,11 +250,13 @@
             tm_here(r, M, sM, rM)
             for side in (0, 1):
                 edge_here(side, MH.at[r], sMH.at[0], rMH.at[r])
-
-        a = [PH[0] * MH[r, 0]] + [PM[x] * M[r, x] for x in range(X)] + [PH[1] * MH[r, 1]]
-        for x in range(X + 1):
+                edge_here(side, IH.at[r], sIH.at[0], rIH.at[r])
+
+        a = [PH[0, n] * MH[r, 0, n] for n in (0, 1)]
+        a = a + [PM[x] * M[r, x] for x in range(X)] + [PH[1, n] * MH[r, 1, n] for n in (0, 1)]
+        for x in range(X + 3):
             TX[slot, x] = jnp.sqrt(a[x] * a[x + 1])
-        for x in range(X):
+        for x in range(X + 2):
             mid = a[x + 1]
             zp = jnp.where(zi < Z - 1, jnp.sqrt(mid * after(mid, 0)), 0.0)
             yp = jnp.where(yi < Y - 1, jnp.sqrt(mid * after(mid, 1)), 0.0)
@@ -242,7 +268,7 @@
             TYM[slot, x] = ym
             RC[slot, x] = 1.0 / (C[x] + (TX[slot, x] + TX[slot, x + 1] + zp + zm + yp + ym))
         rate = column(SM[r], 0)
-        Q[slot] = jnp.dot(put_rows, pick_cols * rate, precision=EXACT).reshape(X, Z, Y)
+        Q[slot] = jnp.dot(put_rows, pick_cols * rate, precision=EXACT).reshape(X + 2, Z, Y)
 
     def start_step(r):
         slot = lax.rem(r, 2)
@@ -252,28 +278,62 @@
             tm_here(r, I, sI, rI)
 
         for x in range(X):
-            B[x] = C[x] * PB[r * ITERS, x] + Q[slot, x] + I[r, x]
-
-    def sweep(r, k):
+            B[x + 1] = C[x + 1] * PB[r * ITERS, x] + Q[slot, x + 1] + I[r, x]
+
+    def layer(k, x):
+        if x < 0:
+            return HP[k, 0, x + 2]
+        return HP[k, 1, x - X] if x >= X else PB[k, x]
+
+    def relaxed(slot, k, x):
+        n = x + 1
+        p = layer(k, x)
+        total = B[n] + TX[slot, n] * layer(k, x - 1) + TX[slot, n + 1] * layer(k, x + 1)
+        total = total + TZP[slot, n] * after(p, 0) + TZM[slot, n] * before(p, 0)
+        total = total + TYP[slot, n] * after(p, 1) + TYM[slot, n] * before(p, 1)
+        return total * RC[slot, n]
+
+    def sweep_wide(r, k):
+        slot = lax.rem(r, 2)
+        for x in range(1, X - 1):
+            PB[k + 1, x] = relaxed(slot, k, x)
+        for side in (0, 1):
+            edge_here(side, HP.at[k], sHP.at[k], rHP.at[k])
+            x = edge[side]
+            PB[k + 1, x] = relaxed(slot, k, x)
+            x = (-1, X)[side]
+            near = HP[k, side, 1 - side]
+            B[x + 1] = C[x + 1] * near + Q[slot, x + 1] + IH[r, side]
+            HP[k + 1, side, 1 - side] = relaxed(slot, k, x)
+
+    def near_edge(side, k):
+        return rdma(
+            PB.at[k, edge[side]], HP.at[k, 1 - side, side], sHP.at[k, side], rHP.at[k, 1 - side],
+            (t, beside[side]),
+        )
+
+    def sweep_plain(r, k):
         slot = lax.rem(r, 2)
         for n, x in enumerate(order):
-            if x == 0:
-                edge_here(0, HP.at[k], sHP.at[k], rHP.at[k])
-                left = HP[k, 0]
-            else:
-                left = PB[k, x - 1]
-            if x == X - 1:
-                edge_here(1, HP.at[k], sHP.at[k], rHP.at[k])
-                right = HP[k, 1]
-            else:
-                right = PB[k, x + 1]
-            p = PB[k, x]
-            total = B[x] + TX[slot, x] * left + TX[slot, x + 1] * right
-            total = total + TZP[slot, x] * after(p, 0) + TZM[slot, x] * before(p, 0)
-            total = total + TYP[slot, x] * after(p, 1) + TYM[slot, x] * before(p, 1)
-            PB[k + 1, x] = total * RC[slot, x]
+            PB[k + 1, x] = relaxed(slot, k, x)
             if n < 2:
-                send_edge(n, PB.at[k + 1, x], HP.at[k + 1], sHP.at[k + 1], rHP.at[k + 1])
+                @pl.when(has[n])
+                def _():
+                    near_edge(n, k + 1).start()
+
+    def sweep_last(r, k):
+        slot = lax.rem(r, 2)
+        for x in range(1, X - 1):
+            PB[k + 1, x] = relaxed(slot, k, x)
+        for side in (0, 1):
+            @pl.when(has[side])
+            def _():
+                near = HP.at[k, side, 1 - side]
+                rdma(near, near, sHP.at[k, side], rHP.at[k, side], (t, beside[side])).wait_recv()
+
+            x = edge[side]
+            PB[k + 1, x] = relaxed(slot, k, x)
+            send_edge(side, PB.at[k + 1, two[side]], HP.at[k + 1], sHP.at[k + 1], rHP.at[k + 1])
 
     parts = ((0, 0, X), (1, 1, X - 2), (2, 0, 1), (3, X - 1, 1))
 
@@ -303,7 +363,7 @@
             return flux * jnp.where(flux > 0, fi, fj)
 
         def p_of(x):
-            return HP[k, 0] if x < 0 else (HP[k, 1] if x >= X else PB[k, x])
+            return layer(k, x)
 
         def f_of(x):
             return HF[r, 0] if x < 0 else (HF[r, 1] if x >= X else FE[r, x])
@@ -319,11 +379,11 @@
             p = p_of(x)
             f = f_of(x)
             s = SB[r, x]
-            q = Q[slot, x]
-            out = face(TX[slot, x + 1], p, p_of(x + 1), f, f_of(x + 1))
-            out = out - face(TX[slot, x], p_of(x - 1), p, f_of(x - 1), f)
-            cz = face(TZP[slot, x], p, after(p, 0), f, after(f, 0))
-            cy = face(TYP[slot, x], p, after(p, 1), f, after(f, 1))
+            q = Q[slot, x + 1]
+            out = face(TX[slot, x + 2], p, p_of(x + 1), f, f_of(x + 1))
+            out = out - face(TX[slot, x + 1], p_of(x - 1), p, f_of(x - 1), f)
+            cz = face(TZP[slot, x + 1], p, after(p, 0), f, after(f, 0))
+            cy = face(TYP[slot, x + 1], p, after(p, 1), f, after(f, 1))
             out = out + (cz - before(cz, 0)) + (cy - before(cy, 1))
             gained = jnp.maximum(q, 0.0) * (1.0 - s) - jnp.maximum(-q, 0.0) * f - out
             s = s + G[x] * gained
@@ -346,13 +406,19 @@
 
     for side in (0, 1):
         edge_here(side, PH, sPH, rPH)
+
+        @pl.when(has[side])
+        def _():
+            storage = C.at[(0, X + 1)[side]]
+            rdma(storage, storage, sC.at[side], rC.at[side], (t, beside[side])).wait_recv()
     coef(0)
     ES[...] = jnp.zeros(ES.shape, jnp.float32)
 
     def step(r, carry):
         k = r * ITERS
         start_step(r)
-        sweep(r, k)
+        sweep_wide(r, k)
+        sweep_plain(r, k + 1)
 
         @pl.when(r > 0)
         def _():
@@ -362,12 +428,12 @@
         def _():
             pass_on(r + 1)
 
-        for j in range(1, ITERS):
-            sweep(r, k + j)
-            if j == 1:
-                @pl.when(r < R - 1)
-                def _():
-                    coef(r + 1)
+        sweep_last(r, k + 2)
+
+        @pl.when(r < R - 1)
+        def _():
+            coef(r + 1)
+
         put_out(r, 0)
         seen = jnp.dot(pick_rows, PB[k + ITERS].reshape(X * Z, Y), precision=EXACT)
         predicted = jnp.sum(seen * pick_cols, axis=1, keepdims=True)
@@ -400,14 +466,28 @@
     mis[...] = result * (1.0 / (R * W))
 
     for side in (0, 1):
-        edge_sent(side, M.at[t, edge[side]], MH.at[t], sMH.at[0], rMH.at[t])
-        edge_sent(side, PM.at[edge[side]], PH, sPH, rPH)
+        edge_sent(side, M.at[t, two[side]], MH.at[t], sMH.at[0], rMH.at[t])
+        edge_sent(side, I.at[t, edge[side]], IH.at[t], sIH.at[0], rIH.at[t])
+        edge_sent(side, PM.at[two[side]], PH, sPH, rPH)
+
+        @pl.when(has[side])
+        def _():
+            storage_edge(side).wait_send()
 
         def sent_k(k, c):
-            edge_sent(side, PB.at[k, edge[side]], HP.at[k], sHP.at[k], rHP.at[k])
+            k = k * ITERS
+            edge_sent(side, PB.at[k, two[side]], HP.at[k], sHP.at[k], rHP.at[k])
             return c
 
-        lax.fori_loop(0, K + 1, sent_k, 0)
+        lax.fori_loop(0, R + 1, sent_k, 0)
+
+        def sent_n(r, c):
+            @pl.when(has[side])
+            def _():
+                near_edge(side, r * ITERS + 2).wait_send()
+            return c
+
+        lax.fori_loop(0, R, sent_n, 0)
 
         def sent_r(r, c):
             edge_sent(side, FE.at[r, edge[side]], HF.at[r], sHF.at[r], rHF.at[r])
@@ -417,11 +497,15 @@
                 rdma(
                     MH.at[r, side], MH.at[r, side], fMH.at[r, side], rMH.at[r, side], (mate, i)
                 ).wait_send()
+                rdma(
+                    IH.at[r, side], IH.at[r, side], fIH.at[r, side], rIH.at[r, side], (mate, i)
+                ).wait_send()
             return c
 
         lax.fori_loop(0, R, sent_r, 0)
         for d, peer in targets():
-            edge_sent(side, M.at[t, edge[side]], MH.at[t], sMH.at[d + 1], rMH.at[t], peer)
+            edge_sent(side, M.at[t, two[side]], MH.at[t], sMH.at[d + 1], rMH.at[t], peer)
+            edge_sent(side, I.at[t, edge[side]], IH.at[t], sIH.at[d + 1], rIH.at[t], peer)
 
     def sent_on(r, c):
         @pl.when(passes_on(r))
@@ -469,6 +553,7 @@
     f32 = jnp.float32
     cell = (Z, Y)
     block = (X, Z, Y)
+    wide = (X + 2, Z, Y)
 
     def buf(*shape):
         return pltpu.VMEM(shape, f32)
@@ -483,17 +568,18 @@
         in_specs=[anyspace] * 6 + [pl.BlockSpec(memory_space=pltpu.SMEM)] + [vmem] * 2,
         out_specs=(vmem, anyspace, anyspace),
         scratch_shapes=[
-            buf(*block), pltpu.VMEM(block, jnp.int32),
-            buf(T, *block), buf(T, *block), buf(T, W, 128), buf(T, 2, *cell), buf(2, *cell),
-            buf(K + 1, 2, *cell), buf(T, 2, *cell), buf(K + 1, *block), buf(T + 1, *block),
-            buf(T + 1, *block), buf(2, X + 1, *cell), buf(2, *block), buf(2, *block),
-            buf(2, *block), buf(2, *block), buf(2, *block), buf(*block), buf(*block), buf(*block),
-            buf(*block), buf(2, *block), buf(8, 128), buf(N, 8, 128), buf(T, 8, 128), buf(W, 1),
+            buf(*block), pltpu.VMEM(block, jnp.int32), buf(T, 2, *cell),
+            buf(T, *block), buf(T, *block), buf(T, W, 128), buf(T, 2, 2, *cell), buf(2, 2, *cell),
+            buf(K + 1, 2, 2, *cell), buf(T, 2, *cell), buf(K + 1, *block), buf(T + 1, *block),
+            buf(T + 1, *block), buf(2, X + 3, *cell), buf(2, *wide), buf(2, *wide),
+            buf(2, *wide), buf(2, *wide), buf(2, *wide), buf(*wide), buf(*block), buf(*block),
+            buf(*wide), buf(2, *wide), buf(8, 128), buf(N, 8, 128), buf(T, 8, 128), buf(W, 1),
             dma((T,)), dma((T,)), dma((T,)), dma((T,)), dma((T,)), dma((T,)),
             dma((T, 2)), dma((T, 2)), dma((2,)), dma((2,)), dma((K + 1, 2)), dma((K + 1, 2)),
             dma((T, 2)), dma((T, 2)), dma((T, 4)), dma((T, 4)), dma((4,)),
             dma((N,)), dma((N,)), dma((T,)), dma((T,)),
-            dma((T,)), dma((T,)), dma((T, 2)), dma((6,)),
+            dma((T,)), dma((T,)), dma((T, 2)), dma((6,)), dma((T, 2)), dma((T, 2)), dma((T, 2)),
+            dma((2,)), dma((2,)),
         ],
         compiler_params=pltpu.CompilerParams(
             has_side_effects=True, collective_id=0

time: 72.9 us -> 78.2 us (1.073)
  Pallas kernels: 66 us -> 71.3 us
    pallas_call x1, Pallas kernels: 66 us -> 71.3 us  [body(): pl.pallas_call(functools.partial(kernel, T, N), out_shape=(jax.ShapeDtype...]
where the time goes in v3:
time: 78.2 us; the launch traced here: 78 us
  Pallas kernels  71.3 us (91%)
  local copies, waits for them, and re-layouts  5.95 us (8%)
    pallas_call x1, Pallas kernels, body(): pl.pallas_call(functools.partial(kernel, T, N), out_shape=(jax.ShapeDtype...  71.3 us
    unnamed x12, local copies, waits for them, and re-layouts  4.06 us

profile of v3, /device:TPU:0, one launch (start us, length us, event | category | flops | bytes accessed | tf_op | source)
XLA Modules:
  0.0 78.0 jit_solution(11118177310483017213)
XLA Ops:
  0.6 0.0 copy-start.4
  0.6 0.6 copy-done.4
  1.3 0.0 copy-start.1
  1.3 0.0 copy-start.2
  1.3 0.0 copy-start.3
  1.3 0.5 copy-done.1
  1.8 0.2 copy-done.2
  2.0 0.0 copy-done.3
  2.0 0.1 copy.17
  2.1 0.6 pad.4.small
  2.7 71.3 %shard_map.121 = (f32[8,128]{1,0:T(8,128)}, f32[1,4,4,32,256]{4,3,2,1,0:T(8,128)}, f32[1,4,4,32,256]{4,3,2,1,0:T(8,128)}) custom-call(f32[4,4,32,256]{3,2,1,0:T(8,128)} %perm.1, f32[1,4,32,256]{3,2,1,0:T(8,128)} %mult.1, f32[1,4,32,256]{3,2,1,0:T(8,128)} %infl.1, f32[4,32,256]{2,1,0:T(8,128)} %p0.1, f32[4,32,256]{2,1,0:T(8,128)} %s0.1, s32[4,32,256]{2,1,0:T(8,128)} %ids.1, ...), custom_call_target="tpu_custom_call" | custom-call | tf_op jit(solution)/shard_map/pallas_call | solution.py:565
  74.0 1.2 %slice_bitcast_fusion = f32[4]{0:T(128)} fusion(f32[8,128]{1,0:T(8,128)} %get-tuple-element.6), kind=kLoop, calls=%fused_computation.8 | loop fusion | bytes 32 | tf_op jit(solution)/shard_map/squeeze | solution.py:591
  75.2 0.0 copy-start
  75.2 1.9 %copy.20 = f32[1,4,4,32,256]{4,3,2,1,0:T(8,128)} copy(f32[1,4,4,32,256]{4,3,2,1,0:T(8,128)} %get-tuple-element.15) | data formatting | bytes 1048576
  77.2 0.0 copy-done
  77.2 0.8 %copy.21 = f32[1,4,4,32,256]{4,3,2,1,0:T(8,128)} copy(f32[1,4,4,32,256]{4,3,2,1,0:T(8,128)S(1)} %copy-done) | data formatting | bytes 1048576
  (2 shorter events, 0.0 us)
Async XLA Ops:
  0.6 0.7 copy-start.4
  1.3 0.5 copy-start.1
  1.3 0.7 copy-start.2
  1.3 0.7 copy-start.3
  75.2 1.9 %copy-start = (f32[1,4,4,32,256]{4,3,2,1,0:T(8,128)S(1)}, f32[1,4,4,32,256]{4,3,2,1,0:T(8,128)}, u32[]{:S(2)}) copy-start(f32[1,4,4,32,256]{4,3,2,1,0:T(8,128)} %get-tuple-element.16) | copy-start | bytes 1572868
